TPU v7x, 512 devices: a whole 4x4x16 slice. The times are simulated.
512 devices in a mesh: tbl: 32 (over z, core), grp: 16 (over y, x).
Axes of the slice: x: 4, y: 4, z: 16, core: 2. Of those that a mesh axis runs over, the one named last changes fastest.
Arguments:
- codes: bfloat16 [32, 4096, 256], P('tbl', 'grp'), may hold values from -4 to 4
- row_scales: float32 [32, 4096], P('tbl', 'grp'), may hold values from 0.25 to 16
- history_lengths: int32 [512, 32], P(None, 'tbl'), may hold values from 1 to 32, as said below
- history_ids: int32 [512, 32, 32], P(None, 'tbl'), may hold values from 0 to 4095, as said below
- query_items: int32 [512, 32], P(None, 'tbl'), may hold values from 0 to 4095, as said below
- slot_tables: int32 [32], replicated, may hold values from 0 to 31, each once
Outputs:
- pooled: bfloat16 [512, 32, 256], P(('tbl', 'grp'))
Inputs may be any that keep to these rules, and one draw needn't show every extreme that they name: `history_lengths`: the largest length, 32, occurs in every draw. `history_ids`: entries at positions at or beyond the history's length are row ids too, and are to be ignored. query_items[b, s] equals history_ids[b, s, h] for some h below history_lengths[b, s].
All inputs are finite; a program needn't handle non-finite values.
Results may differ from a plain program's by a relative error of at most 0.004.
Values may be sent and summed in bfloat16 or wider, within the bound.
No kernel may reach another device: no remote copies, remote signals or barrier semaphores. Data moves between devices by JAX's collectives and lax.ppermute only.
A program may use at most 64 MiB of HBM per device.

v0:
```python
import jax
import jax.numpy as jnp
from jax import lax
from jax.sharding import PartitionSpec as P


def cut_along(value, dim, devices):
    lengths = value.shape
    blocks = value.reshape(*lengths[:dim], devices, lengths[dim] // devices, *lengths[dim + 1 :])
    return jnp.moveaxis(blocks, dim, 0)


def summed_on_arrival(value, axis, dim):
    blocks = cut_along(value, dim, lax.axis_size(axis))
    arrived = lax.all_to_all(blocks, axis, split_axis=0, concat_axis=0, tiled=True)
    return arrived.astype(jnp.float32).sum(axis=0)


def filled_up(lines, devices):
    spare = -lines.shape[0] % devices
    if not spare:
        return lines
    return jnp.concatenate([lines, jnp.zeros((spare, *lines.shape[1:]), lines.dtype)])


def in_order(blocks, dim):
    lengths = list(blocks.shape[1:])
    lengths[dim] *= blocks.shape[0]
    return jnp.moveaxis(blocks, 0, dim).reshape(lengths)


def from_everyone(value, axis):
    devices = lax.axis_size(axis)
    return lax.all_to_all(
        jnp.broadcast_to(value[None], (devices, *value.shape)), axis, 0, 0, tiled=True
    )


def gathered_copies(value, axis, dim):
    return in_order(from_everyone(value, axis), dim)


def nested_sum(value, axes):
    lines = value.reshape(-1, value.shape[-1])
    own = summed_on_arrival(filled_up(lines, lax.axis_size(axes)), axes, 0)
    whole = gathered_copies(own.astype(jnp.bfloat16), axes, 0)
    return whole[: len(lines)].reshape(value.shape).astype(jnp.float32)


def per_device(codes, row_scales, history_lengths, history_ids, query_items, slot_tables):
    slot_count, row_count, emb_width = codes.shape
    batch_rows, _, history = history_ids.shape
    tbl_count = lax.axis_size("tbl")
    grp_count = lax.axis_size("grp")
    owned_rows = batch_rows // (tbl_count * grp_count)
    grp_index = lax.axis_index("grp")
    offset = grp_index * row_count
    query_local = query_items - offset
    query_owned = (query_local >= 0) & (query_local < row_count)
    query_index = jnp.clip(query_local, 0, row_count - 1)
    found = jnp.take(codes[0], query_index[:, 0], axis=0).astype(jnp.float32)
    factor = jnp.take(row_scales[0], query_index[:, 0], axis=0)
    code_parts = [jnp.where(query_owned[:, 0, None], found, 0.0)]
    scale_parts = [jnp.where(query_owned[:, 0], factor, 0.0)]
    query_codes = jnp.stack(code_parts, axis=1)
    query_scales = jnp.stack(scale_parts, axis=1)
    query = nested_sum((query_codes * query_scales[..., None]).astype(jnp.bfloat16), "grp")
    positions = jnp.arange(history, dtype=jnp.int32)
    row_iota = jnp.arange(row_count, dtype=jnp.int32)
    table_rows = codes.astype(jnp.float32)
    block_count = 8
    block_rows = batch_rows // block_count

    def partial_value(block):
        block_ids, block_lengths, block_query = block
        local = block_ids - offset
        live = positions[None, None, :] < block_lengths[:, :, None]
        local = jnp.where(live, local, -1)
        peaks, masses, sums = ([], [], [])
        rows_f = table_rows[0]
        factor = row_scales[0]
        counts = jnp.sum(
            (local[:, 0, :, None] == row_iota[None, None, :]).astype(jnp.float32), axis=1
        )
        raw = jnp.dot(block_query[:, 0], rows_f.T, precision=lax.Precision.HIGHEST)
        score = raw * factor[None, :] / emb_width
        named = counts > 0.0
        peak = jnp.max(jnp.where(named, score, -1e30), axis=1)
        weight = jnp.where(
            named,
            counts * jnp.exp(jnp.where(named, score, 0.0) - jnp.where(named, peak[:, None], 0.0)),
            0.0,
        )
        peaks.append(peak)
        masses.append(jnp.sum(weight, axis=1))
        sums.append(jnp.dot(weight * factor[None, :], rows_f, precision=lax.Precision.HIGHEST))
        return (jnp.stack(peaks, axis=1), jnp.stack(masses, axis=1), jnp.stack(sums, axis=1))

    block_peaks, block_masses, block_sums = lax.map(
        partial_value,
        (
            history_ids.reshape(block_count, block_rows, slot_count, history),
            history_lengths.reshape(block_count, block_rows, slot_count),
            query.reshape(block_count, block_rows, slot_count, emb_width),
        ),
    )
    lead = (tbl_count, grp_count, owned_rows)
    peaks = block_peaks.reshape(lead + (slot_count,))
    masses = block_masses.reshape(lead + (slot_count,))
    sums = block_sums.reshape(lead + (slot_count, emb_width))
    got_peaks, got_masses, got_sums = (
        lax.all_to_all(peaks, "grp", split_axis=1, concat_axis=1, tiled=True),
        lax.all_to_all(masses, "grp", split_axis=1, concat_axis=1, tiled=True),
        lax.all_to_all(sums, "grp", split_axis=1, concat_axis=1, tiled=True),
    )
    peak = jnp.max(got_peaks, axis=1)
    factor = jnp.exp(got_peaks - peak[:, None])
    mass = jnp.sum(got_masses * factor, axis=1)
    weighted = jnp.sum(got_sums * factor[..., None], axis=1)
    pooled_slot = (weighted / mass[..., None]).astype(jnp.bfloat16)
    outgoing = jnp.transpose(pooled_slot, (1, 0, 2, 3))
    arrived = lax.all_to_all(outgoing, "tbl", split_axis=1, concat_axis=1, tiled=True)
    arranged = arrived.reshape(owned_rows, tbl_count * slot_count, emb_width)
    inverse = jnp.argsort(slot_tables)
    return jnp.take(arranged, inverse, axis=1)


def solution(mesh):
    placed = (
        P("tbl", "grp", None),
        P("tbl", "grp"),
        P(None, "tbl"),
        P(None, "tbl", None),
        P(None, "tbl"),
        P(),
    )
    return jax.shard_map(
        per_device,
        mesh=mesh,
        in_specs=placed,
        out_specs=P(("tbl", "grp"), None, None),
        check_vma=False,
    )
```

profile of v0, /device:TPU:1, one launch (start us, length us, event | category | flops | bytes accessed | tf_op | source)
XLA Modules:
  0.0 118.9 jit_solution(13400554463243109967)
XLA Ops:
  0.0 0.7 and_reduce_fusion
  0.8 3.5 %gather_fusion.1 = f32[512]{0:T(512)S(1)} fusion(f32[256]{0:T(256)S(1)} %bitcast.59, s32[1024]{0:T(1024)S(1)} %pad_clamp_fusion.1), kind=kCustom, calls=%fused_computation.1 | custom fusion | bytes 6144 | tf_op jit(solution)/shard_map/jit(_take)/gather | solution.py:62
  4.5 2.0 %gather_fusion = bf16[512,256]{1,0:T(8,128)(2,1)S(1)} fusion(bf16[256,256]{1,0:T(8,128)(2,1)S(1)} %bitcast.62, s32[1024]{0:T(1024)S(1)} %pad_clamp_fusion.1), kind=kCustom, calls=%fused_computation | custom fusion | bytes 526336 | tf_op jit(solution)/shard_map/jit(_take)/gather | solution.py:61
  6.8 14.9 %all_to_all.30 = bf16[16,32,256]{2,1,0:T(8,128)(2,1)S(1)} all-to-all(bf16[16,32,256]{2,1,0:T(8,128)(2,1)S(1)} %multiply_convert_fusion), channel_id=1, replica_groups=mesh['tbl'=32,'grp'=16] {'grp'}, dimensions={0} | all-to-all | bytes 524288 | tf_op jit(solution)/shard_map/all_to_all | solution.py:15
  21.7 0.7 broadcast_in_dim.105
  22.5 3.7 %all-to-all-start.1 = ((bf16[16,32,256]{2,1,0:T(8,128)(2,1)}), bf16[16,32,256]{2,1,0:T(8,128)(2,1)S(1)}, u32[]{:S(2)}, u32[]{:S(2)}) async-start(bf16[16,32,256]{2,1,0:T(8,128)(2,1)} %broadcast_in_dim.105), calls=%async_computation.1 | async-start | bytes 524288 | tf_op jit(solution)/shard_map/all_to_all | solution.py:34
  26.2 0.5 broadcast.153
  26.7 0.7 reduce.17
  27.6 6.1 %all-to-all-done.1 = bf16[16,32,256]{2,1,0:T(8,128)(2,1)S(1)} async-done(((bf16[16,32,256]{2,1,0:T(8,128)(2,1)}), bf16[16,32,256]{2,1,0:T(8,128)(2,1)S(1)}, u32[]{:S(2)}, u32[]{:S(2)}) %all-to-all-start.1) | async-done | bytes 262176 | tf_op jit(solution)/shard_map/all_to_all | solution.py:34
  33.6 0.5 reshape.213
  34.2 13.6 %while.15 = (s32[]{:T(128)}, f32[8,64,1]{1,2,0:T(1,128)S(1)}, f32[8,64,1]{1,2,0:T(1,128)S(1)}, f32[8,64,1,256]{3,1,2,0:T(8,128)S(1)}, s32[8,64,1]{1,2,0:T(1,128)...) while((s32[]{:T(128)}, f32[8,64,1]{1,2,0:T(1,128)S(1)}, ...), condition=%wide.region_6.7_spmd.clone, body=%wide.region_2.6_spmd.clone.sunk | while | flops 102537088 | bytes 1276037 | solution.py:99
  34.3 0.6 convert_reduce_fusion.2
  34.9 0.5 fusion.25
  35.4 0.3 fusion.27
  36.0 0.6 convert_reduce_fusion.2
  36.6 0.5 fusion.25
  37.7 0.6 convert_reduce_fusion.2
  38.3 0.5 fusion.25
  39.4 0.6 convert_reduce_fusion.2
  40.0 0.5 fusion.25
  41.1 0.6 convert_reduce_fusion.2
  41.7 0.5 fusion.25
  42.8 0.6 convert_reduce_fusion.2
  43.4 0.5 fusion.25
  44.5 0.6 convert_reduce_fusion.2
  45.1 0.5 fusion.25
  46.2 0.6 convert_reduce_fusion.2
  46.8 0.5 fusion.25
  47.8 0.5 broadcast.154
  48.3 0.7 reduce.18
  49.1 0.7 copy.18
  49.7 3.5 %all-to-all-start.3 = ((f32[32,16,1,1]{0,3,2,1:T(1,128)}), f32[32,16,1,1]{0,3,2,1:T(1,128)S(1)}, u32[]{:S(2)}, u32[]{:S(2)}) async-start(f32[32,16,1,1]{0,3,2,1:T(1,128)} %copy.18), calls=%async_computation.3 | async-start | bytes 16384 | tf_op jit(solution)/shard_map/all_to_all | solution.py:112
  53.2 0.7 reduce.19
  54.0 0.7 copy.19
  54.7 5.0 %all-to-all-done.3 = f32[32,16,1,1]{0,3,2,1:T(1,128)S(1)} async-done(((f32[32,16,1,1]{0,3,2,1:T(1,128)}), f32[32,16,1,1]{0,3,2,1:T(1,128)S(1)}, u32[]{:S(2)}, u32[]{:S(2)}) %all-to-all-start.3) | async-done | bytes 2080 | tf_op jit(solution)/shard_map/all_to_all | solution.py:112
  59.6 3.5 %all-to-all-start.4 = ((f32[32,16,1,1]{0,3,2,1:T(1,128)}), f32[32,16,1,1]{0,3,2,1:T(1,128)S(1)}, u32[]{:S(2)}, u32[]{:S(2)}) async-start(f32[32,16,1,1]{0,3,2,1:T(1,128)} %copy.19), calls=%async_computation.4 | async-start | bytes 16384 | tf_op jit(solution)/shard_map/all_to_all | solution.py:113
  63.1 1.7 %sort.17 = (s32[32]{0:T(128)}, s32[32]{0:T(128)S(1)}) sort(s32[32]{0:T(128)S(1)} %copy-done.4, s32[32]{0:T(128)S(1)} %iota.10), dimensions={0}, to_apply=%region_0.1 | sort | flops 160 | bytes 512 | tf_op jit(solution)/shard_map/jit(argsort)/sort | solution.py:124
  64.8 1.1 copy.17
  65.9 3.5 %all-to-all-done.4 = f32[32,16,1,1]{0,3,2,1:T(1,128)S(1)} async-done(((f32[32,16,1,1]{0,3,2,1:T(1,128)}), f32[32,16,1,1]{0,3,2,1:T(1,128)S(1)}, u32[]{:S(2)}, u32[]{:S(2)}) %all-to-all-start.4) | async-done | bytes 2080 | tf_op jit(solution)/shard_map/all_to_all | solution.py:113
  69.4 3.6 %all-to-all-start.2 = ((f32[32,16,1,1,256]{4,0,3,2,1:T(8,128)}), f32[32,16,1,1,256]{4,0,3,2,1:T(8,128)S(1)}, u32[]{:S(2)}, u32[]{:S(2)}) async-start(f32[32,16,1,1,256]{4,0,3,2,1:T(8,128)} %copy.17), calls=%async_computation.2 | async-start | bytes 1048576 | tf_op jit(solution)/shard_map/all_to_all | solution.py:114
  73.1 8.8 %all-to-all-done.2 = f32[32,16,1,1,256]{4,0,3,2,1:T(8,128)S(1)} async-done(((f32[32,16,1,1,256]{4,0,3,2,1:T(8,128)}), f32[32,16,1,1,256]{4,0,3,2,1:T(8,128)S(1)}, u32[]{:S(2)}, u32[]{:S(2)}) %all-to-all-start.2) | async-done | bytes 524320 | tf_op jit(solution)/shard_map/all_to_all | solution.py:114
  82.2 0.5 broadcast.156
  82.7 0.7 reduce.20
  83.4 0.6 reshape.269
  84.0 21.8 %all-to-all-start.5 = ((bf16[32,2,128]{2,1,0:T(2,128)(2,1)}), bf16[32,2,128]{2,1,0:T(2,128)(2,1)S(1)}, u32[]{:S(2)}, u32[]{:S(2)}) async-start(bf16[32,2,128]{2,1,0:T(2,128)(2,1)} %reshape.269), calls=%async_computation.5 | async-start | bytes 32768 | tf_op jit(solution)/shard_map/all_to_all | solution.py:122
  105.9 11.7 %all-to-all-done.5 = bf16[32,2,128]{2,1,0:T(2,128)(2,1)S(1)} async-done(((bf16[32,2,128]{2,1,0:T(2,128)(2,1)}), bf16[32,2,128]{2,1,0:T(2,128)(2,1)S(1)}, u32[]{:S(2)}, u32[]{:S(2)}) %all-to-all-start.5) | async-done | bytes 16416 | tf_op jit(solution)/shard_map/all_to_all | solution.py:122
  117.6 0.6 gather_fusion.2
  118.2 0.7 bitcast_select_fusion.1
  (82 shorter events, 6.0 us)
Async XLA Ops:
  0.0 0.7 copy-start
  0.7 3.8 %copy-start.1 = (bf16[1,256,256]{2,1,0:T(8,128)(2,1)S(1)}, bf16[1,256,256]{2,1,0:T(8,128)(2,1)}, u32[]{:S(2)}) copy-start(bf16[1,256,256]{2,1,0:T(8,128)(2,1)} %param.8) | copy-start | bytes 393220
  22.5 4.3 %copy-start.3 = (s32[512,1]{0,1:T(1,128)S(1)}, s32[512,1]{0,1:T(1,128)}, u32[]{:S(2)}) copy-start(s32[512,1]{0,1:T(1,128)} %param.10) | copy-start | bytes 6148
  22.5 5.0 %copy-start.2 = (s32[512,1,32]{0,2,1:T(8,128)S(1)}, s32[512,1,32]{0,2,1:T(8,128)}, u32[]{:S(2)}) copy-start(s32[512,1,32]{0,2,1:T(8,128)} %param.11) | copy-start | bytes 196612
  22.5 11.2 %all-to-all-start.1 = ((bf16[16,32,256]{2,1,0:T(8,128)(2,1)}), bf16[16,32,256]{2,1,0:T(8,128)(2,1)S(1)}, u32[]{:S(2)}, u32[]{:S(2)}) async-start(bf16[16,32,256]{2,1,0:T(8,128)(2,1)} %broadcast_in_dim.105), calls=%async_computation.1 | async-start | bytes 524288 | tf_op jit(solution)/shard_map/all_to_all | solution.py:34
  34.2 28.9 %copy-start.4 = (s32[32]{0:T(128)S(1)}, s32[32]{0:T(128)}, u32[]{:S(2)}) copy-start(s32[32]{0:T(128)} %param.13) | copy-start | bytes 388
  49.7 9.9 %all-to-all-start.3 = ((f32[32,16,1,1]{0,3,2,1:T(1,128)}), f32[32,16,1,1]{0,3,2,1:T(1,128)S(1)}, u32[]{:S(2)}, u32[]{:S(2)}) async-start(f32[32,16,1,1]{0,3,2,1:T(1,128)} %copy.18), calls=%async_computation.3 | async-start | bytes 16384 | tf_op jit(solution)/shard_map/all_to_all | solution.py:112
  59.6 9.8 %all-to-all-start.4 = ((f32[32,16,1,1]{0,3,2,1:T(1,128)}), f32[32,16,1,1]{0,3,2,1:T(1,128)S(1)}, u32[]{:S(2)}, u32[]{:S(2)}) async-start(f32[32,16,1,1]{0,3,2,1:T(1,128)} %copy.19), calls=%async_computation.4 | async-start | bytes 16384 | tf_op jit(solution)/shard_map/all_to_all | solution.py:113
  69.4 12.5 %all-to-all-start.2 = ((f32[32,16,1,1,256]{4,0,3,2,1:T(8,128)}), f32[32,16,1,1,256]{4,0,3,2,1:T(8,128)S(1)}, u32[]{:S(2)}, u32[]{:S(2)}) async-start(f32[32,16,1,1,256]{4,0,3,2,1:T(8,128)} %copy.17), calls=%async_computation.2 | async-start | bytes 1048576 | tf_op jit(solution)/shard_map/all_to_all | solution.py:114
  84.0 33.5 %all-to-all-start.5 = ((bf16[32,2,128]{2,1,0:T(2,128)(2,1)}), bf16[32,2,128]{2,1,0:T(2,128)(2,1)S(1)}, u32[]{:S(2)}, u32[]{:S(2)}) async-start(bf16[32,2,128]{2,1,0:T(2,128)(2,1)} %reshape.269), calls=%async_computation.5 | async-start | bytes 32768 | tf_op jit(solution)/shard_map/all_to_all | solution.py:122
where the time goes:
time: 119 us
  starting transfers between devices  36 us (30%)
  waiting for transfers between devices  35.1 us (29%)
  blocking collectives  14.9 us (13%)
  other arithmetic  13.1 us (11%)
  local copies, waits for them, and re-layouts  12.9 us (11%)
  matrix products  6.38 us (5%)
    all_to_all x1, starting transfers between devices, per_device(): lax.all_to_all(outgoing, 'tbl', split_axis=1, concat_axis=1, tiled=True)  21.8 us
    all_to_all x1, blocking collectives, summed_on_arrival(): lax.all_to_all(blocks, axis, split_axis=0, concat_axis=0, tiled=True)  14.9 us
    all_to_all x1, waiting for transfers between devices, per_device(): lax.all_to_all(outgoing, 'tbl', split_axis=1, concat_axis=1, tiled=True)  11.7 us
    all_to_all x1, waiting for transfers between devices, per_device(): lax.all_to_all(sums, 'grp', split_axis=1, concat_axis=1, tiled=True)  8.84 us
    all_to_all x1, waiting for transfers between devices, from_everyone(): lax.all_to_all(jnp.broadcast_to(value[None], (devices, *value.shape)), ax...  6.05 us
    all_to_all x1, waiting for transfers between devices, per_device(): lax.all_to_all(peaks, 'grp', split_axis=1, concat_axis=1, tiled=True)  4.96 us
    reduce_sum x8, other arithmetic, partial_value(): jnp.sum((local[:, 0, :, None] == row_iota[None, None, :]).astype(jnp.floa...  4.46 us
    dot_general x8, matrix products, partial_value(): raw = jnp.dot(block_query[:, 0], rows_f.T, precision=lax.Precision.HIGHEST)  3.76 us
  transfers between devices with their start and end apart: 5, of which 5 were waited for; matrix products, arithmetic and copies ran while one was open for 5% of the time, Pallas kernels for 0%

commit v1 on v0

v1 whole, which is shorter than its diff:
```python
import jax
import jax.numpy as jnp
from jax import lax
from jax.experimental import pallas as pl
from jax.experimental.pallas import tpu as pltpu
from jax.sharding import PartitionSpec as P

F32 = jnp.float32
BF16 = jnp.bfloat16
VMEM = pl.BlockSpec(memory_space=pltpu.VMEM)
SMEM = pl.BlockSpec(memory_space=pltpu.SMEM)
SCALE_ROWS = 8


def pack_kernel(codes_ref, scales_ref, out_ref, block_ref, sems):
    copies, _, width = out_ref.shape
    rows = codes_ref.shape[0]
    scale = scales_ref[...]
    high = scale.astype(BF16)
    rest = scale - high.astype(F32)
    middle = rest.astype(BF16)
    low = (rest - middle.astype(F32)).astype(BF16)
    place = lax.broadcasted_iota(jnp.int32, (SCALE_ROWS, width), 0)
    terms = jnp.where(
        place == 0,
        high.astype(F32),
        jnp.where(place == 1, middle.astype(F32), jnp.where(place == 2, low.astype(F32), 0.0)),
    ).astype(BF16)
    block_ref[:rows, :] = codes_ref[...]
    block_ref[rows:, :] = terms
    moves = [
        pltpu.make_async_copy(block_ref, out_ref.at[copy], sems.at[copy]) for copy in range(copies)
    ]
    for move in moves:
        move.start()
    for move in moves:
        move.wait()


def count_kernel(grp_ref, ids_ref, lengths_ref, items_ref, counts_ref, target_ref):
    history, batch = ids_ref.shape
    samples, table_rows = counts_ref.shape
    grp_count = batch // samples
    ids = ids_ref[...]
    items = items_ref[...]
    extra = jnp.concatenate(
        [
            lengths_ref[...],
            lax.shift_right_logical(items, 6),
            jnp.bitwise_and(items, 63),
            jnp.zeros((5, batch), jnp.int32),
        ],
        axis=0,
    )
    digits = jnp.concatenate(
        [lax.shift_right_logical(ids, 6), jnp.bitwise_and(ids, 63), extra], axis=0
    )
    digits = digits.astype(F32).astype(BF16)
    sample = lax.broadcasted_iota(jnp.int32, (samples, batch), 0)
    column = lax.broadcasted_iota(jnp.int32, (samples, batch), 1)
    chosen = jnp.where(column == sample * grp_count + grp_ref[0], 1.0, 0.0).astype(BF16)
    own = lax.dot_general(chosen, digits, (((1,), (1,)), ((), ())), preferred_element_type=F32)
    own_ids = own[:, :history] * 64.0 + own[:, history : 2 * history]
    own_lengths = own[:, 2 * history : 2 * history + 1]
    own_items = own[:, 2 * history + 1 : 2 * history + 2] * 64.0 + own[:, 2 * history + 2 : 2 * history + 3]
    position = lax.broadcasted_iota(jnp.int32, (samples, history), 1).astype(F32)
    own_ids = jnp.where(position < own_lengths, own_ids, -1.0)
    lane = lax.broadcasted_iota(jnp.int32, (8, 128), 1).astype(F32)
    for first in range(0, samples, 8):
        names = [
            jnp.broadcast_to(own_ids[first : first + 8, h : h + 1], (8, 128)) for h in range(history)
        ]
        item = jnp.broadcast_to(own_items[first : first + 8], (8, 128))

        def tile(k, carry):
            row = lane + (k * 128).astype(F32)
            total = jnp.zeros((8, 128), F32)
            for h in range(history):
                total = total + jnp.where(names[h] == row, 1.0, 0.0)
            at = pl.ds(pl.multiple_of(k * 128, 128), 128)
            counts_ref[first : first + 8, at] = total
            target_ref[first : first + 8, at] = jnp.where(item == row, 1.0, 0.0)
            return carry

        lax.fori_loop(0, table_rows // 128, tile, 0, unroll=2)


def pool_kernel(table_ref, counts_ref, target_ref, out_ref, score_ref):
    blocks, height, width = table_ref.shape
    rows = height - SCALE_ROWS
    samples = counts_ref.shape[0]

    def scales(block):
        terms = table_ref[block, rows:, :].astype(F32)
        return terms[0:1] + (terms[1:2] + terms[2:3])

    query = jnp.zeros((samples, width), F32)
    factor = jnp.zeros((samples, rows), F32)
    for block in range(blocks):
        target = target_ref[:, block * rows : (block + 1) * rows]
        query = query + jnp.dot(
            target.astype(BF16), table_ref[block, :rows, :], preferred_element_type=F32
        )
        factor = factor + target * scales(block)
    query = query.astype(BF16)
    factor = jnp.sum(factor, axis=1, keepdims=True) * (1.0 / width)
    top = jnp.full((samples, rows), -1e30, F32)
    for block in range(blocks):
        raw = lax.dot_general(
            query, table_ref[block, :rows, :], (((1,), (1,)), ((), ())), preferred_element_type=F32
        )
        score = raw * scales(block) * factor
        at = slice(block * rows, (block + 1) * rows)
        score = jnp.where(counts_ref[:, at] > 0.0, score, -1e30)
        score_ref[:, at] = score
        top = jnp.maximum(top, score)
    peak = jnp.max(top, axis=1, keepdims=True)
    mass = jnp.zeros((samples, rows), F32)
    pooled = jnp.zeros((2 * samples, width), F32)
    for block in range(blocks):
        at = slice(block * rows, (block + 1) * rows)
        weight = counts_ref[:, at] * jnp.exp(score_ref[:, at] - peak)
        mass = mass + weight
        scaled = weight * scales(block)
        high = scaled.astype(BF16)
        low = (scaled - high.astype(F32)).astype(BF16)
        pooled = pooled + jnp.dot(
            jnp.concatenate([high, low], axis=0),
            table_ref[block, :rows, :],
            preferred_element_type=F32,
        )
    mass = jnp.sum(mass, axis=1, keepdims=True)
    out_ref[...] = ((pooled[:samples] + pooled[samples:]) / mass).astype(out_ref.dtype)


def order_kernel(tables_ref, pooled_ref, out_ref):
    slots = pooled_ref.shape[0]
    table = lax.broadcasted_iota(jnp.int32, (slots, slots), 0)
    place = jnp.where(table == tables_ref[...], 1.0, 0.0).astype(BF16)
    out_ref[0] = jnp.dot(place, pooled_ref[...], preferred_element_type=F32).astype(BF16)


def per_device(codes, row_scales, history_lengths, history_ids, query_items, slot_tables):
    _, rows, width = codes.shape
    batch, _, history = history_ids.shape
    tbl_count = lax.axis_size("tbl")
    grp_count = lax.axis_size("grp")
    samples = batch // grp_count
    table_rows = rows * grp_count
    packed = pl.pallas_call(
        pack_kernel,
        out_shape=jax.ShapeDtypeStruct((grp_count, rows + SCALE_ROWS, width), BF16),
        in_specs=[VMEM, VMEM],
        out_specs=pl.BlockSpec(memory_space=pltpu.HBM),
        scratch_shapes=[
            pltpu.VMEM((rows + SCALE_ROWS, width), BF16),
            pltpu.SemaphoreType.DMA((grp_count,)),
        ],
        compiler_params=pltpu.CompilerParams(vmem_limit_bytes=16 << 20),
        name="pack",
    )(codes[0], row_scales)
    table = lax.all_to_all(packed, "grp", split_axis=0, concat_axis=0, tiled=True)
    grp = lax.axis_index("grp").astype(jnp.int32).reshape(1)
    counts, target = pl.pallas_call(
        count_kernel,
        out_shape=[
            jax.ShapeDtypeStruct((samples, table_rows), F32),
            jax.ShapeDtypeStruct((samples, table_rows), F32),
        ],
        in_specs=[SMEM, VMEM, VMEM, VMEM],
        out_specs=[VMEM, VMEM],
        cost_estimate=pl.CostEstimate(flops=100_000_000, bytes_accessed=1_000_000, transcendentals=0),
        compiler_params=pltpu.CompilerParams(vmem_limit_bytes=16 << 20),
        name="count",
    )(grp, history_ids[:, 0, :].T, history_lengths.T, query_items.T)
    pooled = pl.pallas_call(
        pool_kernel,
        out_shape=jax.ShapeDtypeStruct((samples, width), BF16),
        in_specs=[VMEM, VMEM, VMEM],
        out_specs=VMEM,
        scratch_shapes=[pltpu.VMEM((samples, table_rows), F32)],
        compiler_params=pltpu.CompilerParams(vmem_limit_bytes=16 << 20),
        name="pool",
    )(table, counts, target)
    arrived = lax.all_to_all(pooled, "tbl", split_axis=0, concat_axis=0, tiled=True)
    return pl.pallas_call(
        order_kernel,
        out_shape=jax.ShapeDtypeStruct((1, tbl_count, width), BF16),
        in_specs=[VMEM, VMEM],
        out_specs=VMEM,
        compiler_params=pltpu.CompilerParams(vmem_limit_bytes=16 << 20),
        name="order",
    )(slot_tables.reshape(1, tbl_count), arrived)


def solution(mesh):
    placed = (
        P("tbl", "grp", None),
        P("tbl", "grp"),
        P(None, "tbl"),
        P(None, "tbl", None),
        P(None, "tbl"),
        P(),
    )
    return jax.shard_map(
        per_device,
        mesh=mesh,
        in_specs=placed,
        out_specs=P(("tbl", "grp"), None, None),
        check_vma=False,
    )
```

time: 119 us -> 79 us (0.66)
  starting transfers between devices: 36 us -> 7.7 us
  blocking collectives: 14.9 us -> 34.6 us
  waiting for transfers between devices: 35.1 us -> 22.5 us
  other arithmetic: 13.1 us -> 0.65 us
  Pallas kernels: 0 us -> 9.72 us
  local copies, waits for them, and re-layouts: 12.9 us -> 3.51 us
  matrix products: 6.38 us -> 0 us
    all_to_all x5 -> x1, starting transfers between devices: 36 us -> 7.7 us  [per_device(): lax.all_to_all(packed, 'grp', split_axis=0, concat_axis=0, tiled=True)]
    all_to_all x1, blocking collectives: 14.9 us -> 34.6 us  [per_device(): lax.all_to_all(pooled, 'tbl', split_axis=0, concat_axis=0, tiled=True)]
    all_to_all x5 -> x1, waiting for transfers between devices: 35.1 us -> 22.5 us  [per_device(): lax.all_to_all(packed, 'grp', split_axis=0, concat_axis=0, tiled=True)]
    pallas_call x0 -> x4, Pallas kernels: none -> 9.72 us  [the longest x1 3.42 us: per_device(): pl.pallas_call(count_kernel, out_shape=[jax.ShapeDtypeStruct((samples, ta...]
    dot_general x16 -> x0, matrix products: 6.38 us -> none  [the longest x8 3.76 us: partial_value(): raw = jnp.dot(block_query[:, 0], rows_f.T, precision=lax.Precision.HIGHEST)]
    reduce_sum x19 -> x0, other arithmetic: 6.16 us -> none  [the longest x8 4.46 us: partial_value(): jnp.sum((local[:, 0, :, None] == row_iota[None, None, :]).astype(jnp.floa...]
    gather x4 -> x0, local copies, waits for them, and re-layouts: 6.16 us -> none  [the longest x2 3.58 us: per_device(): factor = jnp.take(row_scales[0], query_index[:, 0], axis=0)]
    reshape x6 -> x0, local copies, waits for them, and re-layouts: 2.67 us -> none  [the longest x1 1.1 us: per_device(): sums = block_sums.reshape(lead + (slot_count, emb_width))]
  transfers between devices with their start and end apart: 5 -> 1, of which waited for: 5 -> 1; matrix products, arithmetic and copies ran while one was open for 5% -> 0% of each run, Pallas kernels for 0% -> 4%
where the time goes in v1:
time: 79 us; the launch traced here: 78.8 us
  blocking collectives  34.6 us (44%)
  waiting for transfers between devices  22.5 us (28%)
  Pallas kernels  9.72 us (12%)
  starting transfers between devices  7.7 us (10%)
  local copies, waits for them, and re-layouts  3.51 us (4%)
    all_to_all x1, blocking collectives, per_device(): lax.all_to_all(pooled, 'tbl', split_axis=0, concat_axis=0, tiled=True)  34.6 us
    all_to_all x1, waiting for transfers between devices, per_device(): lax.all_to_all(packed, 'grp', split_axis=0, concat_axis=0, tiled=True)  22.5 us
    all_to_all x1, starting transfers between devices, per_device(): lax.all_to_all(packed, 'grp', split_axis=0, concat_axis=0, tiled=True)  7.7 us
    pallas_call x1, Pallas kernels, per_device(): pl.pallas_call(count_kernel, out_shape=[jax.ShapeDtypeStruct((samples, ta...  3.42 us
    pallas_call x1, Pallas kernels, per_device(): pl.pallas_call(pack_kernel, out_shape=jax.ShapeDtypeStruct((grp_count, ro...  2.97 us
    unnamed x17, local copies, waits for them, and re-layouts  2.97 us
    pallas_call x1, Pallas kernels, per_device(): pl.pallas_call(pool_kernel, out_shape=jax.ShapeDtypeStruct((samples, widt...  2.6 us
  transfers between devices with their start and end apart: 1, of which 1 were waited for; matrix products, arithmetic and copies ran while one was open for 0% of the time, Pallas kernels for 4%

profile of v1, /device:TPU:1, one launch (start us, length us, event | category | flops | bytes accessed | tf_op | source)
XLA Modules:
  0.0 78.8 jit_solution(14221081799834523282)
XLA Ops:
  0.0 0.0 copy-start.1
  0.0 0.9 %copy-done.1 = bf16[1,256,256]{2,1,0:T(8,128)(2,1)S(1)} copy-done((bf16[1,256,256]{2,1,0:T(8,128)(2,1)S(1)}, bf16[1,256,256]{2,1,0:T(8,128)(2,1)}, u32[]{:S(2)}) %copy-start.1) | copy-done | bytes 131096
  0.9 0.0 copy-start.2
  0.9 0.7 copy-done.2
  1.6 3.0 %pack.1 = bf16[16,264,256]{2,1,0:T(8,128)(2,1)S(1)} custom-call(bf16[256,256]{1,0:T(8,128)(2,1)S(1)} %bitcast.12, f32[1,256]{1,0:T(1,128)S(1)} %copy-done.2), custom_call_target="tpu_custom_call" | custom-call | tf_op jit(solution)/shard_map/pack/pallas_call | solution.py:150
  4.6 0.0 copy-start
  4.6 1.3 %copy-done = bf16[16,264,256]{2,1,0:T(8,128)(2,1)} copy-done((bf16[16,264,256]{2,1,0:T(8,128)(2,1)}, bf16[16,264,256]{2,1,0:T(8,128)(2,1)S(1)}, u32[]{:S(2)}) %copy-start) | copy-done | bytes 2162712
  5.9 0.0 copy-start.4
  5.9 0.0 copy-start.5
  5.9 0.0 copy-start.6
  5.9 7.7 %all-to-all-start = ((bf16[16,264,256]{2,1,0:T(8,128)(2,1)}), bf16[16,264,256]{2,1,0:T(8,128)(2,1)S(1)}, u32[]{:S(2)}, u32[]{:S(2)}) async-start(bf16[16,264,256]{2,1,0:T(8,128)(2,1)} %copy-done), calls=%async_computation | async-start | bytes 4325376 | tf_op jit(solution)/shard_map/all_to_all | solution.py:162
  13.6 0.0 copy-start.3
  13.7 0.0 copy-done.4
  13.7 0.0 copy-done.5
  13.7 0.0 copy-done.6
  13.7 3.4 %count.1 = (f32[32,4096]{1,0:T(8,128)S(1)}, f32[32,4096]{1,0:T(8,128)S(1)}) custom-call(s32[1]{0:T(128)} %bitcast.2.grp_ref, s32[32,512]{1,0:T(8,128)S(1)} %bitcast.16, s32[1,512]{1,0:T(1,128)S(1)} %bitcast.17, s32[1,512]{1,0:T(1,128)S(1)} %bitcast.18), custom_call_target="tpu_custom_call" | custom-call | flops 100000000 | bytes 1000000 | tf_op jit(solution)/shard_map/count/pallas_call | solution.py:164
  17.1 22.5 %all-to-all-done.table_ref = bf16[16,264,256]{2,1,0:T(8,128)(2,1)S(1)} async-done(((bf16[16,264,256]{2,1,0:T(8,128)(2,1)}), bf16[16,264,256]{2,1,0:T(8,128)(2,1)S(1)}, u32[]{:S(2)}, u32[]{:S(2)}) %all-to-all-start) | async-done | bytes 2162720 | tf_op jit(solution)/shard_map/all_to_all | solution.py:162
  39.6 2.6 %pool.1 = bf16[32,256]{1,0:T(8,128)(2,1)S(1)} custom-call(bf16[16,264,256]{2,1,0:T(8,128)(2,1)S(1)} %all-to-all-done.table_ref, f32[32,4096]{1,0:T(8,128)S(1)} %get-tuple-element.7.counts_ref, f32[32,4096]{1,0:T(8,128)S(1)} %get-tuple-element.8.target_ref), custom_call_target="tpu_custom_call" | custom-call | tf_op jit(solution)/shard_map/pool/pallas_call | solution.py:176
  42.2 0.5 broadcast
  42.8 0.7 reduce
  43.4 34.6 %all_to_all.16 = bf16[32,2,128]{2,1,0:T(2,128)(2,1)S(1)} all-to-all(bf16[32,2,128]{2,1,0:T(2,128)(2,1)S(1)} %reshape.10), channel_id=1, replica_groups=mesh['tbl'=32,'grp'=16] {'tbl'}, dimensions={0} | all-to-all | bytes 32768 | tf_op jit(solution)/shard_map/all_to_all | solution.py:185
  78.0 0.0 copy-done.3
  78.0 0.7 order.1
  (3 shorter events, 0.0 us)
Async XLA Ops:
  0.0 0.9 %copy-start.1 = (bf16[1,256,256]{2,1,0:T(8,128)(2,1)S(1)}, bf16[1,256,256]{2,1,0:T(8,128)(2,1)}, u32[]{:S(2)}) copy-start(bf16[1,256,256]{2,1,0:T(8,128)(2,1)} %param.6) | copy-start | bytes 393220
  0.9 0.7 copy-start.2
  4.6 1.3 %copy-start = (bf16[16,264,256]{2,1,0:T(8,128)(2,1)}, bf16[16,264,256]{2,1,0:T(8,128)(2,1)S(1)}, u32[]{:S(2)}) copy-start(bf16[16,264,256]{2,1,0:T(8,128)(2,1)S(1)} %pack.1) | copy-start | bytes 6488068
  5.9 7.7 %copy-start.4 = (s32[512,1,32]{0,2,1:T(8,128)S(1)}, s32[512,1,32]{0,2,1:T(8,128)}, u32[]{:S(2)}) copy-start(s32[512,1,32]{0,2,1:T(8,128)} %param.9) | copy-start | bytes 196612
  5.9 7.7 %copy-start.5 = (s32[512,1]{0,1:T(1,128)S(1)}, s32[512,1]{0,1:T(1,128)}, u32[]{:S(2)}) copy-start(s32[512,1]{0,1:T(1,128)} %param.8) | copy-start | bytes 6148
  5.9 7.8 %copy-start.6 = (s32[512,1]{0,1:T(1,128)S(1)}, s32[512,1]{0,1:T(1,128)}, u32[]{:S(2)}) copy-start(s32[512,1]{0,1:T(1,128)} %param.10) | copy-start | bytes 6148
  5.9 33.7 %all-to-all-start = ((bf16[16,264,256]{2,1,0:T(8,128)(2,1)}), bf16[16,264,256]{2,1,0:T(8,128)(2,1)S(1)}, u32[]{:S(2)}, u32[]{:S(2)}) async-start(bf16[16,264,256]{2,1,0:T(8,128)(2,1)} %copy-done), calls=%async_computation | async-start | bytes 4325376 | tf_op jit(solution)/shard_map/all_to_all | solution.py:162
  13.6 64.4 %copy-start.3 = (s32[32]{0:T(128)S(1)}, s32[32]{0:T(128)}, u32[]{:S(2)}) copy-start(s32[32]{0:T(128)} %param.11) | copy-start | bytes 388

commit v2 on v1

--- a/solution.py
+++ b/solution.py
@@ -1,3 +1,5 @@
+import functools
+
 import jax
 import jax.numpy as jnp
 from jax import lax
@@ -9,13 +11,27 @@
 BF16 = jnp.bfloat16
 VMEM = pl.BlockSpec(memory_space=pltpu.VMEM)
 SMEM = pl.BlockSpec(memory_space=pltpu.SMEM)
+HBM = pl.BlockSpec(memory_space=pltpu.HBM)
+SMALL = pltpu.CompilerParams(vmem_limit_bytes=16 << 20)
 SCALE_ROWS = 8
-
-
-def pack_kernel(codes_ref, scales_ref, out_ref, block_ref, sems):
-    copies, _, width = out_ref.shape
-    rows = codes_ref.shape[0]
-    scale = scales_ref[...]
+LANES = 128
+
+
+def rotated(count, first):
+    return [(place + first) % count for place in range(count)]
+
+
+def pack_kernel(codes_ref, scales_ref, out_ref, block_ref, scale_ref, sems):
+    copies = out_ref.shape[0]
+    rows, width = codes_ref.shape
+    fetch = [
+        pltpu.make_async_copy(codes_ref, block_ref.at[pl.ds(0, rows)], sems.at[copies]),
+        pltpu.make_async_copy(scales_ref, scale_ref, sems.at[copies + 1]),
+    ]
+    for move in fetch:
+        move.start()
+    fetch[1].wait()
+    scale = scale_ref[...]
     high = scale.astype(BF16)
     rest = scale - high.astype(F32)
     middle = rest.astype(BF16)
@@ -26,8 +42,8 @@
         high.astype(F32),
         jnp.where(place == 1, middle.astype(F32), jnp.where(place == 2, low.astype(F32), 0.0)),
     ).astype(BF16)
-    block_ref[:rows, :] = codes_ref[...]
     block_ref[rows:, :] = terms
+    fetch[0].wait()
     moves = [
         pltpu.make_async_copy(block_ref, out_ref.at[copy], sems.at[copy]) for copy in range(copies)
     ]
@@ -37,7 +53,7 @@
         move.wait()
 
 
-def count_kernel(grp_ref, ids_ref, lengths_ref, items_ref, counts_ref, target_ref):
+def count_kernel(tbl_order, grp_ref, ids_ref, lengths_ref, items_ref, counts_ref, target_ref):
     history, batch = ids_ref.shape
     samples, table_rows = counts_ref.shape
     grp_count = batch // samples
@@ -58,6 +74,7 @@
     digits = digits.astype(F32).astype(BF16)
     sample = lax.broadcasted_iota(jnp.int32, (samples, batch), 0)
     column = lax.broadcasted_iota(jnp.int32, (samples, batch), 1)
+    sample = (sample + tbl_order[0]) % samples
     chosen = jnp.where(column == sample * grp_count + grp_ref[0], 1.0, 0.0).astype(BF16)
     own = lax.dot_general(chosen, digits, (((1,), (1,)), ((), ())), preferred_element_type=F32)
     own_ids = own[:, :history] * 64.0 + own[:, history : 2 * history]
@@ -85,7 +102,7 @@
         lax.fori_loop(0, table_rows // 128, tile, 0, unroll=2)
 
 
-def pool_kernel(table_ref, counts_ref, target_ref, out_ref, score_ref):
+def pool_kernel(grp_order, table_ref, counts_ref, target_ref, out_ref, score_ref):
     blocks, height, width = table_ref.shape
     rows = height - SCALE_ROWS
     samples = counts_ref.shape[0]
@@ -94,10 +111,13 @@
         terms = table_ref[block, rows:, :].astype(F32)
         return terms[0:1] + (terms[1:2] + terms[2:3])
 
+    def columns(block):
+        return slice(grp_order[block] * rows, (grp_order[block] + 1) * rows)
+
     query = jnp.zeros((samples, width), F32)
     factor = jnp.zeros((samples, rows), F32)
     for block in range(blocks):
-        target = target_ref[:, block * rows : (block + 1) * rows]
+        target = target_ref[:, columns(block)]
         query = query + jnp.dot(
             target.astype(BF16), table_ref[block, :rows, :], preferred_element_type=F32
         )
@@ -110,7 +130,7 @@
             query, table_ref[block, :rows, :], (((1,), (1,)), ((), ())), preferred_element_type=F32
         )
         score = raw * scales(block) * factor
-        at = slice(block * rows, (block + 1) * rows)
+        at = columns(block)
         score = jnp.where(counts_ref[:, at] > 0.0, score, -1e30)
         score_ref[:, at] = score
         top = jnp.maximum(top, score)
@@ -118,7 +138,7 @@
     mass = jnp.zeros((samples, rows), F32)
     pooled = jnp.zeros((2 * samples, width), F32)
     for block in range(blocks):
-        at = slice(block * rows, (block + 1) * rows)
+        at = columns(block)
         weight = counts_ref[:, at] * jnp.exp(score_ref[:, at] - peak)
         mass = mass + weight
         scaled = weight * scales(block)
@@ -130,14 +150,21 @@
             preferred_element_type=F32,
         )
     mass = jnp.sum(mass, axis=1, keepdims=True)
-    out_ref[...] = ((pooled[:samples] + pooled[samples:]) / mass).astype(out_ref.dtype)
-
-
-def order_kernel(tables_ref, pooled_ref, out_ref):
-    slots = pooled_ref.shape[0]
+    pooled = ((pooled[:samples] + pooled[samples:]) / mass).astype(out_ref.dtype)
+    for part in range(width // LANES):
+        out_ref[:, part, :] = pooled[:, part * LANES : (part + 1) * LANES]
+
+
+def order_kernel(tbl_order, tables_ref, pooled_ref, out_ref):
+    slots, parts, lanes = pooled_ref.shape
+    first = tbl_order[0]
     table = lax.broadcasted_iota(jnp.int32, (slots, slots), 0)
     place = jnp.where(table == tables_ref[...], 1.0, 0.0).astype(BF16)
-    out_ref[0] = jnp.dot(place, pooled_ref[...], preferred_element_type=F32).astype(BF16)
+    for part in range(parts):
+        rows = pooled_ref[:, part, :]
+        rows = jnp.concatenate([rows[slots - first :], rows[: slots - first]], axis=0)
+        ordered = jnp.dot(place, rows, preferred_element_type=F32).astype(BF16)
+        out_ref[0, :, part * lanes : (part + 1) * lanes] = ordered
 
 
 def per_device(codes, row_scales, history_lengths, history_ids, query_items, slot_tables):
@@ -147,22 +174,32 @@
     grp_count = lax.axis_size("grp")
     samples = batch // grp_count
     table_rows = rows * grp_count
+    grp_order = rotated(grp_count, 10)
+    tbl_order = rotated(tbl_count, tbl_count // 2)
+    along_grp = [[t * grp_count + g for g in grp_order] for t in range(tbl_count)]
+    along_tbl = [[t * grp_count + g for t in tbl_order] for g in range(grp_count)]
+
+    def exchange(blocks, groups):
+        return lax.all_to_all(
+            blocks, ("tbl", "grp"), 0, 0, axis_index_groups=groups, tiled=True
+        )
+
     packed = pl.pallas_call(
         pack_kernel,
         out_shape=jax.ShapeDtypeStruct((grp_count, rows + SCALE_ROWS, width), BF16),
-        in_specs=[VMEM, VMEM],
-        out_specs=pl.BlockSpec(memory_space=pltpu.HBM),
+        in_specs=[HBM, HBM],
+        out_specs=HBM,
         scratch_shapes=[
             pltpu.VMEM((rows + SCALE_ROWS, width), BF16),
-            pltpu.SemaphoreType.DMA((grp_count,)),
+            pltpu.VMEM((1, rows), F32),
+            pltpu.SemaphoreType.DMA((grp_count + 2,)),
         ],
-        compiler_params=pltpu.CompilerParams(vmem_limit_bytes=16 << 20),
         name="pack",
     )(codes[0], row_scales)
-    table = lax.all_to_all(packed, "grp", split_axis=0, concat_axis=0, tiled=True)
+    table = exchange(packed, along_grp)
     grp = lax.axis_index("grp").astype(jnp.int32).reshape(1)
     counts, target = pl.pallas_call(
-        count_kernel,
+        functools.partial(count_kernel, tbl_order),
         out_shape=[
             jax.ShapeDtypeStruct((samples, table_rows), F32),
             jax.ShapeDtypeStruct((samples, table_rows), F32),
@@ -170,25 +207,25 @@
         in_specs=[SMEM, VMEM, VMEM, VMEM],
         out_specs=[VMEM, VMEM],
         cost_estimate=pl.CostEstimate(flops=100_000_000, bytes_accessed=1_000_000, transcendentals=0),
-        compiler_params=pltpu.CompilerParams(vmem_limit_bytes=16 << 20),
+        compiler_params=SMALL,
         name="count",
     )(grp, history_ids[:, 0, :].T, history_lengths.T, query_items.T)
     pooled = pl.pallas_call(
-        pool_kernel,
-        out_shape=jax.ShapeDtypeStruct((samples, width), BF16),
+        functools.partial(pool_kernel, grp_order),
+        out_shape=jax.ShapeDtypeStruct((samples, width // LANES, LANES), BF16),
         in_specs=[VMEM, VMEM, VMEM],
         out_specs=VMEM,
         scratch_shapes=[pltpu.VMEM((samples, table_rows), F32)],
-        compiler_params=pltpu.CompilerParams(vmem_limit_bytes=16 << 20),
+        compiler_params=SMALL,
         name="pool",
     )(table, counts, target)
-    arrived = lax.all_to_all(pooled, "tbl", split_axis=0, concat_axis=0, tiled=True)
+    arrived = exchange(pooled, along_tbl)
     return pl.pallas_call(
-        order_kernel,
+        functools.partial(order_kernel, tbl_order),
         out_shape=jax.ShapeDtypeStruct((1, tbl_count, width), BF16),
         in_specs=[VMEM, VMEM],
         out_specs=VMEM,
-        compiler_params=pltpu.CompilerParams(vmem_limit_bytes=16 << 20),
+        compiler_params=SMALL,
         name="order",
     )(slot_tables.reshape(1, tbl_count), arrived)
 

time: 79 us -> 65.6 us (0.83)
  blocking collectives: 34.6 us -> 25 us
  local copies, waits for them, and re-layouts: 3.51 us -> 0.02 us
  starting transfers between devices: 7.7 us -> 9.88 us
  waiting for transfers between devices: 22.5 us -> 20.4 us
    all_to_all x1, blocking collectives: 34.6 us -> 25 us  [exchange(): lax.all_to_all(blocks, ('tbl', 'grp'), 0, 0, axis_index_groups=groups, ti...]
    unnamed x17 -> x8, local copies, waits for them, and re-layouts: 2.97 us -> 0.02 us
    all_to_all x1, starting transfers between devices: 7.7 us -> 9.88 us  [exchange(): lax.all_to_all(blocks, ('tbl', 'grp'), 0, 0, axis_index_groups=groups, ti...]
    all_to_all x1, waiting for transfers between devices: 22.5 us -> 20.4 us  [exchange(): lax.all_to_all(blocks, ('tbl', 'grp'), 0, 0, axis_index_groups=groups, ti...]
  transfers between devices with their start and end apart: 1 -> 1, of which waited for: 1 -> 1; matrix products, arithmetic and copies ran while one was open for 0% -> 0% of each run, Pallas kernels for 4% -> 5%
where the time goes in v2:
time: 65.6 us; the launch traced here: 64.7 us
  blocking collectives  25 us (38%)
  waiting for transfers between devices  20.4 us (31%)
  starting transfers between devices  9.88 us (15%)
  Pallas kernels  9.3 us (14%)
    all_to_all x1, blocking collectives, exchange(): lax.all_to_all(blocks, ('tbl', 'grp'), 0, 0, axis_index_groups=groups, ti...  25 us
    all_to_all x1, waiting for transfers between devices, exchange(): lax.all_to_all(blocks, ('tbl', 'grp'), 0, 0, axis_index_groups=groups, ti...  20.4 us
    all_to_all x1, starting transfers between devices, exchange(): lax.all_to_all(blocks, ('tbl', 'grp'), 0, 0, axis_index_groups=groups, ti...  9.88 us
    pallas_call x1, Pallas kernels, per_device(): pl.pallas_call(functools.partial(count_kernel, tbl_order), out_shape=[jax...  3.42 us
    pallas_call x1, Pallas kernels, per_device(): pl.pallas_call(functools.partial(pool_kernel, grp_order), out_shape=jax.S...  2.69 us
    pallas_call x1, Pallas kernels, per_device(): pl.pallas_call(pack_kernel, out_shape=jax.ShapeDtypeStruct((grp_count, ro...  2.42 us
  transfers between devices with their start and end apart: 1, of which 1 were waited for; matrix products, arithmetic and copies ran while one was open for 0% of the time, Pallas kernels for 5%

profile of v2, /device:TPU:1, one launch (start us, length us, event | category | flops | bytes accessed | tf_op | source)
XLA Modules:
  0.0 64.7 jit_solution(16605811731804908475)
XLA Ops:
  0.0 2.4 %pack.1 = bf16[16,264,256]{2,1,0:T(8,128)(2,1)} custom-call(bf16[256,256]{1,0:T(8,128)(2,1)} %bitcast.12, f32[1,256]{1,0:T(1,128)} %scales_ref.1), custom_call_target="tpu_custom_call" | custom-call | tf_op jit(solution)/shard_map/pack/pallas_call | solution.py:187
  2.4 0.0 copy-start.1
  2.4 0.0 copy-start.2
  2.4 0.0 copy-start.3
  2.5 9.9 %all-to-all-start = ((bf16[16,264,256]{2,1,0:T(8,128)(2,1)}), bf16[16,264,256]{2,1,0:T(8,128)(2,1)S(1)}, u32[]{:S(2)}, u32[]{:S(2)}) async-start(bf16[16,264,256]{2,1,0:T(8,128)(2,1)} %pack.1), calls=%async_computation | async-start | bytes 4325376 | tf_op jit(solution)/shard_map/all_to_all | solution.py:183
  12.3 0.0 copy-start
  12.3 0.0 copy-done.1
  12.4 0.0 copy-done.2
  12.4 0.0 copy-done.3
  12.4 3.4 %count.1 = (f32[32,4096]{1,0:T(8,128)S(1)}, f32[32,4096]{1,0:T(8,128)S(1)}) custom-call(s32[1]{0:T(128)} %bitcast.2.grp_ref, s32[32,512]{1,0:T(8,128)S(1)} %bitcast.9, s32[1,512]{1,0:T(1,128)S(1)} %bitcast.10, s32[1,512]{1,0:T(1,128)S(1)} %bitcast.11), custom_call_target="tpu_custom_call" | custom-call | flops 100000000 | bytes 1000000 | tf_op jit(solution)/shard_map/count/pallas_call | solution.py:201
  15.8 20.4 %all-to-all-done.table_ref = bf16[16,264,256]{2,1,0:T(8,128)(2,1)S(1)} async-done(((bf16[16,264,256]{2,1,0:T(8,128)(2,1)}), bf16[16,264,256]{2,1,0:T(8,128)(2,1)S(1)}, u32[]{:S(2)}, u32[]{:S(2)}) %all-to-all-start) | async-done | bytes 2162720 | tf_op jit(solution)/shard_map/all_to_all | solution.py:183
  36.2 2.7 %pool.1 = bf16[32,2,128]{2,1,0:T(2,128)(2,1)S(1)} custom-call(bf16[16,264,256]{2,1,0:T(8,128)(2,1)S(1)} %all-to-all-done.table_ref, f32[32,4096]{1,0:T(8,128)S(1)} %get-tuple-element.7.counts_ref, f32[32,4096]{1,0:T(8,128)S(1)} %get-tuple-element.8.target_ref), custom_call_target="tpu_custom_call" | custom-call | tf_op jit(solution)/shard_map/pool/pallas_call | solution.py:213
  38.9 25.0 %all_to_all.10.pooled_ref = bf16[32,2,128]{2,1,0:T(2,128)(2,1)S(1)} all-to-all(bf16[32,2,128]{2,1,0:T(2,128)(2,1)S(1)} %pool.1), channel_id=1, replica_groups={{256,272,288,304,320,336,352,368,384,400,416,432,448,464,480,496,0,16,3..., dimensions={0} | all-to-all | bytes 32768 | tf_op jit(solution)/shard_map/all_to_all | solution.py:183
  64.0 0.0 copy-done
  64.0 0.8 %order.1 = bf16[1,32,256]{2,1,0:T(8,128)(2,1)} custom-call(s32[1,32]{1,0:T(1,128)S(1)} %bitcast.8, bf16[32,2,128]{2,1,0:T(2,128)(2,1)S(1)} %all_to_all.10.pooled_ref), custom_call_target="tpu_custom_call" | custom-call | tf_op jit(solution)/shard_map/order/pallas_call | solution.py:223
Async XLA Ops:
  2.4 9.9 %copy-start.1 = (s32[512,1,32]{0,2,1:T(8,128)S(1)}, s32[512,1,32]{0,2,1:T(8,128)}, u32[]{:S(2)}) copy-start(s32[512,1,32]{0,2,1:T(8,128)} %param.9) | copy-start | bytes 196612
  2.4 9.9 %copy-start.2 = (s32[512,1]{0,1:T(1,128)S(1)}, s32[512,1]{0,1:T(1,128)}, u32[]{:S(2)}) copy-start(s32[512,1]{0,1:T(1,128)} %param.8) | copy-start | bytes 6148
  2.4 9.9 %copy-start.3 = (s32[512,1]{0,1:T(1,128)S(1)}, s32[512,1]{0,1:T(1,128)}, u32[]{:S(2)}) copy-start(s32[512,1]{0,1:T(1,128)} %param.10) | copy-start | bytes 6148
  2.5 33.8 %all-to-all-start = ((bf16[16,264,256]{2,1,0:T(8,128)(2,1)}), bf16[16,264,256]{2,1,0:T(8,128)(2,1)S(1)}, u32[]{:S(2)}, u32[]{:S(2)}) async-start(bf16[16,264,256]{2,1,0:T(8,128)(2,1)} %pack.1), calls=%async_computation | async-start | bytes 4325376 | tf_op jit(solution)/shard_map/all_to_all | solution.py:183
  12.3 51.6 %copy-start = (s32[32]{0:T(128)S(1)}, s32[32]{0:T(128)}, u32[]{:S(2)}) copy-start(s32[32]{0:T(128)} %param.11) | copy-start | bytes 388

commit v3 on v2

v3 whole, which is shorter than its diff:
```python
import functools

import jax
import jax.numpy as jnp
from jax import lax
from jax.experimental import pallas as pl
from jax.experimental.pallas import tpu as pltpu
from jax.sharding import PartitionSpec as P

F32 = jnp.float32
BF16 = jnp.bfloat16
VMEM = pl.BlockSpec(memory_space=pltpu.VMEM)
SMEM = pl.BlockSpec(memory_space=pltpu.SMEM)
HBM = pl.BlockSpec(memory_space=pltpu.HBM)
SMALL = pltpu.CompilerParams(vmem_limit_bytes=16 << 20)
SCALE_ROWS = 8
LANES = 128
CHIPS_X = 4
SPARE = 6


def rotated(count, first):
    return [(place + first) % count for place in range(count)]


def pack_kernel(codes_ref, scales_ref, out_ref, block_ref, scale_ref, sems):
    copies = out_ref.shape[0]
    rows, width = codes_ref.shape
    fetch = [
        pltpu.make_async_copy(codes_ref, block_ref.at[pl.ds(0, rows)], sems.at[copies]),
        pltpu.make_async_copy(scales_ref, scale_ref, sems.at[copies + 1]),
    ]
    for move in fetch:
        move.start()
    fetch[1].wait()
    scale = scale_ref[...]
    high = scale.astype(BF16)
    rest = scale - high.astype(F32)
    middle = rest.astype(BF16)
    low = (rest - middle.astype(F32)).astype(BF16)
    place = lax.broadcasted_iota(jnp.int32, (SCALE_ROWS, width), 0)
    terms = jnp.where(
        place == 0,
        high.astype(F32),
        jnp.where(place == 1, middle.astype(F32), jnp.where(place == 2, low.astype(F32), 0.0)),
    ).astype(BF16)
    block_ref[rows:, :] = terms
    fetch[0].wait()
    moves = [
        pltpu.make_async_copy(block_ref, out_ref.at[copy], sems.at[copy]) for copy in range(copies)
    ]
    for move in moves:
        move.start()
    for move in moves:
        move.wait()


def three_terms(value):
    high = value.astype(BF16).astype(F32)
    rest = value - high
    middle = rest.astype(BF16).astype(F32)
    return high, middle, rest - middle


def count_kernel(order, grp_ref, ids_ref, lengths_ref, items_ref, counts_ref, target_ref, names_ref, item_ref):
    tbl_order, y_order, x_order = order
    history, batch = ids_ref.shape
    samples, held = counts_ref.shape
    tbl_count, x_count = len(tbl_order), len(x_order)
    grp_count = batch // tbl_count
    rows = held // x_count
    grp = grp_ref[0]
    y, x = grp // x_count, grp % x_count
    ids = ids_ref[...]
    items = items_ref[...]
    extra = jnp.concatenate(
        [
            lengths_ref[...],
            lax.shift_right_logical(items, 6),
            jnp.bitwise_and(items, 63),
            jnp.zeros((5, batch), jnp.int32),
        ],
        axis=0,
    )
    digits = jnp.concatenate(
        [lax.shift_right_logical(ids, 6), jnp.bitwise_and(ids, 63), extra], axis=0
    )
    digits = digits.astype(F32).astype(BF16)
    sample = lax.broadcasted_iota(jnp.int32, (samples, batch), 0)
    column = lax.broadcasted_iota(jnp.int32, (samples, batch), 1)
    tbl_at = (sample % tbl_count + tbl_order[0]) % tbl_count
    y_at = (sample // tbl_count + y_order[0]) % len(y_order)
    chosen = jnp.where(column == tbl_at * grp_count + y_at * x_count + x, 1.0, 0.0).astype(BF16)
    own = lax.dot_general(chosen, digits, (((1,), (1,)), ((), ())), preferred_element_type=F32)

    def held_at(high, low):
        row = (high * 64.0 + low).astype(jnp.int32)
        owner = row // rows
        block = (owner % x_count - x_order[0] + x_count) % x_count
        return jnp.where(owner // x_count == y, block * rows + row % rows, -1)

    own_lengths = own[:, 2 * history : 2 * history + 1].astype(jnp.int32)
    position = lax.broadcasted_iota(jnp.int32, (samples, history), 1)
    names = held_at(own[:, :history], own[:, history : 2 * history])
    names_ref[...] = jnp.where(position < own_lengths, names, -1)
    item = held_at(
        own[:, 2 * history + 1 : 2 * history + 2], own[:, 2 * history + 2 : 2 * history + 3]
    )
    item_ref[...] = jnp.broadcast_to(item, item_ref.shape)
    lane = lax.broadcasted_iota(jnp.int32, (8, LANES), 1)

    def group(k, carry):
        at = pl.ds(pl.multiple_of(k * 8, 8), 8)
        named = names_ref[at, :]
        named = [jnp.broadcast_to(named[:, h : h + 1], (8, LANES)) for h in range(history)]
        item = item_ref[at, :]
        for first in range(0, held, LANES):
            row = lane + first
            total = jnp.zeros((8, LANES), F32)
            for h in range(history):
                total = total + jnp.where(named[h] == row, 1.0, 0.0)
            counts_ref[at, first : first + LANES] = total
            target_ref[at, first : first + LANES] = jnp.where(item == row, 1.0, 0.0)
        return carry

    lax.fori_loop(0, samples // 8, group, 0)


def query_kernel(table_ref, target_ref, out_ref):
    copies, height, width = out_ref.shape
    blocks = table_ref.shape[0]
    rows = table_ref.shape[1] - SCALE_ROWS
    samples = target_ref.shape[0]
    codes = jnp.zeros((samples, width), F32)
    terms = jnp.zeros((SCALE_ROWS, samples), F32)
    for block in range(blocks):
        target = target_ref[:, block * rows : (block + 1) * rows].astype(BF16)
        codes = codes + jnp.dot(target, table_ref[block, :rows, :], preferred_element_type=F32)
        terms = terms + lax.dot_general(
            table_ref[block, rows:, :],
            target,
            (((1,), (1,)), ((), ())),
            preferred_element_type=F32,
        )
    codes = codes.astype(BF16)
    terms = jnp.concatenate([terms, jnp.zeros((SCALE_ROWS, width - samples), F32)], axis=1)
    terms = terms.astype(BF16)
    for copy in range(copies):
        out_ref[copy, :samples, :] = codes
        out_ref[copy, samples:, :] = terms


def pool_kernel(table_ref, counts_ref, query_ref, out_ref, score_ref):
    blocks, height, width = table_ref.shape
    rows = height - SCALE_ROWS
    samples = counts_ref.shape[0]

    def scales(block):
        terms = table_ref[block, rows:, :].astype(F32)
        return terms[0:1] + (terms[1:2] + terms[2:3])

    def columns(block):
        return slice(block * rows, (block + 1) * rows)

    query = query_ref[0].astype(F32)
    for copy in range(1, query_ref.shape[0]):
        query = query + query_ref[copy].astype(F32)
    factor = query[samples:, :samples]
    factor = (factor[0:1] + (factor[1:2] + factor[2:3])) * (1.0 / width)
    factor = jnp.broadcast_to(factor, (samples, samples)).T
    factor = jnp.concatenate([factor] * (rows // samples), axis=1)
    query = query[:samples].astype(BF16)
    top = jnp.full((samples, rows), -1e30, F32)
    for block in range(blocks):
        raw = lax.dot_general(
            query, table_ref[block, :rows, :], (((1,), (1,)), ((), ())), preferred_element_type=F32
        )
        score = raw * scales(block) * factor
        score = jnp.where(counts_ref[:, columns(block)] > 0.0, score, -1e30)
        score_ref[:, columns(block)] = score
        top = jnp.maximum(top, score)
    peak = jnp.max(top, axis=1, keepdims=True)
    mass = jnp.zeros((samples, rows), F32)
    pooled = jnp.zeros((2 * samples, width), F32)
    for block in range(blocks):
        weight = counts_ref[:, columns(block)] * jnp.exp(score_ref[:, columns(block)] - peak)
        mass = mass + weight
        scaled = weight * scales(block)
        high = scaled.astype(BF16)
        low = (scaled - high.astype(F32)).astype(BF16)
        pooled = pooled + jnp.dot(
            jnp.concatenate([high, low], axis=0),
            table_ref[block, :rows, :],
            preferred_element_type=F32,
        )
    mass = jnp.sum(mass, axis=1, keepdims=True)
    pooled = pooled[:samples] + pooled[samples:]
    high = pooled.astype(BF16).astype(F32)
    low = pooled - high
    lane = lax.broadcasted_iota(jnp.int32, (samples, width), 1)
    for place, term in enumerate(three_terms(peak) + three_terms(mass)):
        low = jnp.where(lane == width - SPARE + place, term, low)
    high = high.astype(BF16)
    low = low.astype(BF16)
    parts = width // LANES
    for part in range(parts):
        out_ref[:, part, :] = high[:, part * LANES : (part + 1) * LANES]
        out_ref[:, parts + part, :] = low[:, part * LANES : (part + 1) * LANES]


def combine_kernel(order, tables_ref, got_ref, out_ref):
    tbl_order, y_order, _ = order
    slots = len(tbl_order)
    parts = got_ref.shape[1] // 2
    pieces = [got_ref[:, part, :].astype(F32) for part in range(2 * parts)]
    last = pieces[-1]
    spare = [last[:, k : k + 1] for k in range(LANES - SPARE, LANES)]
    peak = spare[0] + (spare[1] + spare[2])
    mass = spare[3] + (spare[4] + spare[5])
    lane = lax.broadcasted_iota(jnp.int32, last.shape, 1)
    pieces[-1] = jnp.where(lane < LANES - SPARE, last, 0.0)
    ranges = [slice(k * slots, (k + 1) * slots) for k in range(len(y_order))]
    top = functools.reduce(jnp.maximum, [peak[at] for at in ranges])
    shift = [jnp.exp(peak[at] - top) for at in ranges]
    whole = sum(f * mass[at] for f, at in zip(shift, ranges))
    table = lax.broadcasted_iota(jnp.int32, (slots, slots), 0)
    place = jnp.where(table == tables_ref[...], 1.0, 0.0).astype(BF16)
    first = slots - tbl_order[0]
    for part in range(parts):
        value = pieces[part] + pieces[parts + part]
        rows = sum(f * value[at] for f, at in zip(shift, ranges)) / whole
        rows = jnp.concatenate([rows[first:], rows[:first]], axis=0).astype(BF16)
        ordered = jnp.dot(place, rows, preferred_element_type=F32).astype(BF16)
        out_ref[0, :, part * LANES : (part + 1) * LANES] = ordered


def per_device(codes, row_scales, history_lengths, history_ids, query_items, slot_tables):
    _, rows, width = codes.shape
    batch, _, history = history_ids.shape
    tbl_count = lax.axis_size("tbl")
    grp_count = lax.axis_size("grp")
    x_count = CHIPS_X
    y_count = grp_count // x_count
    samples = batch // x_count
    held = rows * x_count
    tbl_order = rotated(tbl_count, tbl_count // 2)
    y_order = rotated(y_count, y_count // 2)
    x_order = rotated(x_count, x_count // 2)
    order = (tbl_order, y_order, x_order)
    tables, ys, xs = range(tbl_count), range(y_count), range(x_count)

    def device(t, y, x):
        return (t * y_count + y) * x_count + x

    along_x = [[device(t, y, x) for x in x_order] for t in tables for y in ys]
    along_y = [[device(t, y, x) for y in y_order] for t in tables for x in xs]
    to_owner = [[device(t, y, x) for y in y_order for t in tbl_order] for x in xs]

    def exchange(blocks, groups):
        return lax.all_to_all(
            blocks, ("tbl", "grp"), 0, 0, axis_index_groups=groups, tiled=True
        )

    packed = pl.pallas_call(
        pack_kernel,
        out_shape=jax.ShapeDtypeStruct((x_count, rows + SCALE_ROWS, width), BF16),
        in_specs=[HBM, HBM],
        out_specs=HBM,
        scratch_shapes=[
            pltpu.VMEM((rows + SCALE_ROWS, width), BF16),
            pltpu.VMEM((1, rows), F32),
            pltpu.SemaphoreType.DMA((x_count + 2,)),
        ],
        name="pack",
    )(codes[0], row_scales)
    table = exchange(packed, along_x)
    grp = lax.axis_index("grp").astype(jnp.int32).reshape(1)
    counts, target = pl.pallas_call(
        functools.partial(count_kernel, order),
        out_shape=[
            jax.ShapeDtypeStruct((samples, held), F32),
            jax.ShapeDtypeStruct((samples, held), F32),
        ],
        in_specs=[SMEM, VMEM, VMEM, VMEM],
        out_specs=[VMEM, VMEM],
        scratch_shapes=[
            pltpu.VMEM((samples, history), jnp.int32),
            pltpu.VMEM((samples, LANES), jnp.int32),
        ],
        cost_estimate=pl.CostEstimate(flops=100_000_000, bytes_accessed=1_000_000, transcendentals=0),
        compiler_params=SMALL,
        name="count",
    )(grp, history_ids[:, 0, :].T, history_lengths.T, query_items.T)
    masked = pl.pallas_call(
        query_kernel,
        out_shape=jax.ShapeDtypeStruct((y_count, samples + SCALE_ROWS, width), BF16),
        in_specs=[VMEM, VMEM],
        out_specs=VMEM,
        compiler_params=SMALL,
        name="query",
    )(table, target)
    query = exchange(masked, along_y)
    partial = pl.pallas_call(
        pool_kernel,
        out_shape=jax.ShapeDtypeStruct((samples, 2 * (width // LANES), LANES), BF16),
        in_specs=[VMEM, VMEM, VMEM],
        out_specs=VMEM,
        scratch_shapes=[pltpu.VMEM((samples, held), F32)],
        compiler_params=SMALL,
        name="pool",
    )(table, counts, query)
    got = exchange(partial, to_owner)
    return pl.pallas_call(
        functools.partial(combine_kernel, order),
        out_shape=jax.ShapeDtypeStruct((1, tbl_count, width), BF16),
        in_specs=[VMEM, VMEM],
        out_specs=VMEM,
        compiler_params=SMALL,
        name="combine",
    )(slot_tables.reshape(1, tbl_count), got)


def solution(mesh):
    placed = (
        P("tbl", "grp", None),
        P("tbl", "grp"),
        P(None, "tbl"),
        P(None, "tbl", None),
        P(None, "tbl"),
        P(),
    )
    return jax.shard_map(
        per_device,
        mesh=mesh,
        in_specs=placed,
        out_specs=P(("tbl", "grp"), None, None),
        check_vma=False,
    )
```

time: 65.6 us -> 59.2 us (0.902)
  waiting for transfers between devices: 20.4 us -> 0.1 us
  blocking collectives: 25 us -> 42 us
  starting transfers between devices: 9.88 us -> 7.15 us
  local copies, waits for them, and re-layouts: 0.02 us -> 1.34 us
  Pallas kernels: 9.3 us -> 8.22 us
    all_to_all x1, waiting for transfers between devices: 20.4 us -> 0.1 us  [exchange(): lax.all_to_all(blocks, ('tbl', 'grp'), 0, 0, axis_index_groups=groups, ti...]
    all_to_all x1 -> x2, blocking collectives: 25 us -> 42 us  [exchange(): lax.all_to_all(blocks, ('tbl', 'grp'), 0, 0, axis_index_groups=groups, ti...]
    all_to_all x1, starting transfers between devices: 9.88 us -> 7.15 us  [exchange(): lax.all_to_all(blocks, ('tbl', 'grp'), 0, 0, axis_index_groups=groups, ti...]
    unnamed x8, local copies, waits for them, and re-layouts: 0.02 us -> 1.34 us
    pallas_call x4 -> x5, Pallas kernels: 9.3 us -> 8.22 us  [the longest x1 3.54 us: per_device(): pl.pallas_call(functools.partial(count_kernel, order), out_shape=[jax.Sha...]
  transfers between devices with their start and end apart: 1 -> 1, of which waited for: 1 -> 1; matrix products, arithmetic and copies ran while one was open for 0% -> 0% of each run, Pallas kernels for 5% -> 6%
where the time goes in v3:
time: 59.2 us; the launch traced here: 58.9 us
  blocking collectives  42 us (71%)
  Pallas kernels  8.22 us (14%)
  starting transfers between devices  7.15 us (12%)
  local copies, waits for them, and re-layouts  1.34 us (2%)
    all_to_all x2, blocking collectives, exchange(): lax.all_to_all(blocks, ('tbl', 'grp'), 0, 0, axis_index_groups=groups, ti...  42 us
    all_to_all x1, starting transfers between devices, exchange(): lax.all_to_all(blocks, ('tbl', 'grp'), 0, 0, axis_index_groups=groups, ti...  7.15 us
    pallas_call x1, Pallas kernels, per_device(): pl.pallas_call(functools.partial(count_kernel, order), out_shape=[jax.Sha...  3.54 us
    pallas_call x1, Pallas kernels, per_device(): pl.pallas_call(pack_kernel, out_shape=jax.ShapeDtypeStruct((x_count, rows...  1.76 us
    pallas_call x1, Pallas kernels, per_device(): pl.pallas_call(functools.partial(combine_kernel, order), out_shape=jax.Sh...  1.38 us
    unnamed x8, local copies, waits for them, and re-layouts  1.34 us
    pallas_call x1, Pallas kernels, per_device(): pl.pallas_call(pool_kernel, out_shape=jax.ShapeDtypeStruct((samples, 2 *...  1.25 us
  transfers between devices with their start and end apart: 1, of which 1 were waited for; matrix products, arithmetic and copies ran while one was open for 0% of the time, Pallas kernels for 6%

profile of v3, /device:TPU:1, one launch (start us, length us, event | category | flops | bytes accessed | tf_op | source)
XLA Modules:
  0.0 58.9 jit_solution(9128613524304113056)
XLA Ops:
  0.0 1.8 %pack.1 = bf16[4,264,256]{2,1,0:T(8,128)(2,1)} custom-call(bf16[256,256]{1,0:T(8,128)(2,1)} %bitcast.12, f32[1,256]{1,0:T(1,128)} %scales_ref.1), custom_call_target="tpu_custom_call" | custom-call | tf_op jit(solution)/shard_map/pack/pallas_call | solution.py:264
  1.8 0.0 copy-start.1
  1.8 0.0 copy-start.3
  1.8 7.1 %all-to-all-start = ((bf16[4,264,256]{2,1,0:T(8,128)(2,1)}), bf16[4,264,256]{2,1,0:T(8,128)(2,1)S(1)}, u32[]{:S(2)}, u32[]{:S(2)}) async-start(bf16[4,264,256]{2,1,0:T(8,128)(2,1)} %pack.1), calls=%async_computation | async-start | bytes 1081344 | tf_op jit(solution)/shard_map/all_to_all | solution.py:260
  8.9 0.0 copy-start.2
  8.9 0.0 copy-done.1
  8.9 0.0 copy-done.3
  8.9 0.7 %copy-done.2 = s32[512,1]{0,1:T(1,128)S(1)} copy-done((s32[512,1]{0,1:T(1,128)S(1)}, s32[512,1]{0,1:T(1,128)}, u32[]{:S(2)}) %copy-start.2) | copy-done | bytes 2072
  9.6 3.5 %count.1 = (f32[128,1024]{1,0:T(8,128)S(1)}, f32[128,1024]{1,0:T(8,128)S(1)}) custom-call(s32[1]{0:T(128)} %bitcast.2.grp_ref, s32[32,512]{1,0:T(8,128)S(1)} %bitcast.9, s32[1,512]{1,0:T(1,128)S(1)} %bitcast.10, s32[1,512]{1,0:T(1,128)S(1)} %bitcast.11), custom_call_target="tpu_custom_call" | custom-call | flops 100000000 | bytes 1000000 | tf_op jit(solution)/shard_map/count/pallas_call | solution.py:278
  13.2 0.1 all-to-all-done.table_ref
  13.3 0.3 query.1
  13.6 10.3 %all_to_all.15.query_ref = bf16[4,136,256]{2,1,0:T(8,128)(2,1)S(1)} all-to-all(bf16[4,136,256]{2,1,0:T(8,128)(2,1)S(1)} %query.1), channel_id=1, replica_groups={{8,12,0,4},{9,13,1,5},{10,14,2,6},{11,15,3,7},{24,28,16,20},{25,29,17,2..., dimensions={0} | all-to-all | bytes 557056 | tf_op jit(solution)/shard_map/all_to_all | solution.py:260
  23.9 1.2 %pool.1 = bf16[128,4,128]{2,1,0:T(4,128)(2,1)S(1)} custom-call(bf16[4,264,256]{2,1,0:T(8,128)(2,1)S(1)} %all-to-all-done.table_ref, f32[128,1024]{1,0:T(8,128)S(1)} %get-tuple-element.7.counts_ref, bf16[4,136,256]{2,1,0:T(8,128)(2,1)S(1)} %all_to_all.15.query_ref), custom_call_target="tpu_custom_call" | custom-call | tf_op jit(solution)/shard_map/pool/pallas_call | solution.py:303
  25.1 31.7 %all_to_all.16.got_ref = bf16[128,4,128]{2,1,0:T(4,128)(2,1)S(1)} all-to-all(bf16[128,4,128]{2,1,0:T(4,128)(2,1)S(1)} %pool.1), channel_id=1, replica_groups={{264,280,296,312,328,344,360,376,392,408,424,440,456,472,488,504,8,24,4..., dimensions={0} | all-to-all | bytes 262144 | tf_op jit(solution)/shard_map/all_to_all | solution.py:260
  56.8 0.0 copy-start
  56.8 0.7 %copy-done = s32[32]{0:T(128)S(1)} copy-done((s32[32]{0:T(128)S(1)}, s32[32]{0:T(128)}, u32[]{:S(2)}) %copy-start) | copy-done | bytes 152
  57.5 1.4 %combine.1 = bf16[1,32,256]{2,1,0:T(8,128)(2,1)} custom-call(s32[1,32]{1,0:T(1,128)S(1)} %bitcast.8, bf16[128,4,128]{2,1,0:T(4,128)(2,1)S(1)} %all_to_all.16.got_ref), custom_call_target="tpu_custom_call" | custom-call | tf_op jit(solution)/shard_map/combine/pallas_call | solution.py:313
Async XLA Ops:
  1.8 7.2 %copy-start.1 = (s32[512,1,32]{0,2,1:T(8,128)S(1)}, s32[512,1,32]{0,2,1:T(8,128)}, u32[]{:S(2)}) copy-start(s32[512,1,32]{0,2,1:T(8,128)} %param.9) | copy-start | bytes 196612
  1.8 7.2 %copy-start.3 = (s32[512,1]{0,1:T(1,128)S(1)}, s32[512,1]{0,1:T(1,128)}, u32[]{:S(2)}) copy-start(s32[512,1]{0,1:T(1,128)} %param.10) | copy-start | bytes 6148
  1.8 11.5 %all-to-all-start = ((bf16[4,264,256]{2,1,0:T(8,128)(2,1)}), bf16[4,264,256]{2,1,0:T(8,128)(2,1)S(1)}, u32[]{:S(2)}, u32[]{:S(2)}) async-start(bf16[4,264,256]{2,1,0:T(8,128)(2,1)} %pack.1), calls=%async_computation | async-start | bytes 1081344 | tf_op jit(solution)/shard_map/all_to_all | solution.py:260
  8.9 0.7 %copy-start.2 = (s32[512,1]{0,1:T(1,128)S(1)}, s32[512,1]{0,1:T(1,128)}, u32[]{:S(2)}) copy-start(s32[512,1]{0,1:T(1,128)} %param.8) | copy-start | bytes 6148
  56.8 0.7 %copy-start = (s32[32]{0:T(128)S(1)}, s32[32]{0:T(128)}, u32[]{:S(2)}) copy-start(s32[32]{0:T(128)} %param.11) | copy-start | bytes 388

commit v4 on v3

--- a/solution.py
+++ b/solution.py
@@ -16,7 +16,6 @@
 SCALE_ROWS = 8
 LANES = 128
 CHIPS_X = 4
-SPARE = 6
 
 
 def rotated(count, first):
@@ -55,14 +54,19 @@
         move.wait()
 
 
-def three_terms(value):
-    high = value.astype(BF16).astype(F32)
-    rest = value - high
-    middle = rest.astype(BF16).astype(F32)
-    return high, middle, rest - middle
-
-
-def count_kernel(order, grp_ref, ids_ref, lengths_ref, items_ref, counts_ref, target_ref, names_ref, item_ref):
+def count_kernel(
+    order,
+    grp_ref,
+    ids_ref,
+    lengths_ref,
+    items_ref,
+    tables_ref,
+    counts_ref,
+    target_ref,
+    place_ref,
+    names_ref,
+    item_ref,
+):
     tbl_order, y_order, x_order = order
     history, batch = ids_ref.shape
     samples, held = counts_ref.shape
@@ -124,6 +128,8 @@
         return carry
 
     lax.fori_loop(0, samples // 8, group, 0)
+    table = lax.broadcasted_iota(jnp.int32, place_ref.shape, 0)
+    place_ref[...] = jnp.where(table == tables_ref[...], 1.0, 0.0)
 
 
 def query_kernel(table_ref, target_ref, out_ref):
@@ -195,43 +201,36 @@
         )
     mass = jnp.sum(mass, axis=1, keepdims=True)
     pooled = pooled[:samples] + pooled[samples:]
-    high = pooled.astype(BF16).astype(F32)
-    low = pooled - high
-    lane = lax.broadcasted_iota(jnp.int32, (samples, width), 1)
-    for place, term in enumerate(three_terms(peak) + three_terms(mass)):
-        low = jnp.where(lane == width - SPARE + place, term, low)
-    high = high.astype(BF16)
-    low = low.astype(BF16)
-    parts = width // LANES
+    lane = lax.broadcasted_iota(jnp.int32, (samples, LANES), 1)
+    last = jnp.where(lane == 0, peak, mass)
+    size = out_ref.shape[1]
+    for block in range(out_ref.shape[0]):
+        out_ref[block, :, :width] = pooled[block * size : (block + 1) * size]
+        out_ref[block, :, width:] = last[block * size : (block + 1) * size]
+
+
+def merge_kernel(got_ref, out_ref):
+    count = got_ref.shape[0]
+    width = got_ref.shape[2] - LANES
+    peaks = [got_ref[k, :, width : width + 1] for k in range(count)]
+    top = functools.reduce(jnp.maximum, peaks)
+    shift = [jnp.exp(peak - top) for peak in peaks]
+    mass = sum(f * got_ref[k, :, width + 1 : width + 2] for k, f in enumerate(shift))
+    pooled = sum(f * got_ref[k, :, :width] for k, f in enumerate(shift)) / mass
+    pooled = pooled.astype(BF16)
+    for part in range(width // LANES):
+        out_ref[:, part, :] = pooled[:, part * LANES : (part + 1) * LANES]
+
+
+def order_kernel(tbl_order, place_ref, pooled_ref, out_ref):
+    slots, parts, lanes = pooled_ref.shape
+    first = slots - tbl_order[0]
+    place = place_ref[...].astype(BF16)
     for part in range(parts):
-        out_ref[:, part, :] = high[:, part * LANES : (part + 1) * LANES]
-        out_ref[:, parts + part, :] = low[:, part * LANES : (part + 1) * LANES]
-
-
-def combine_kernel(order, tables_ref, got_ref, out_ref):
-    tbl_order, y_order, _ = order
-    slots = len(tbl_order)
-    parts = got_ref.shape[1] // 2
-    pieces = [got_ref[:, part, :].astype(F32) for part in range(2 * parts)]
-    last = pieces[-1]
-    spare = [last[:, k : k + 1] for k in range(LANES - SPARE, LANES)]
-    peak = spare[0] + (spare[1] + spare[2])
-    mass = spare[3] + (spare[4] + spare[5])
-    lane = lax.broadcasted_iota(jnp.int32, last.shape, 1)
-    pieces[-1] = jnp.where(lane < LANES - SPARE, last, 0.0)
-    ranges = [slice(k * slots, (k + 1) * slots) for k in range(len(y_order))]
-    top = functools.reduce(jnp.maximum, [peak[at] for at in ranges])
-    shift = [jnp.exp(peak[at] - top) for at in ranges]
-    whole = sum(f * mass[at] for f, at in zip(shift, ranges))
-    table = lax.broadcasted_iota(jnp.int32, (slots, slots), 0)
-    place = jnp.where(table == tables_ref[...], 1.0, 0.0).astype(BF16)
-    first = slots - tbl_order[0]
-    for part in range(parts):
-        value = pieces[part] + pieces[parts + part]
-        rows = sum(f * value[at] for f, at in zip(shift, ranges)) / whole
-        rows = jnp.concatenate([rows[first:], rows[:first]], axis=0).astype(BF16)
+        rows = pooled_ref[:, part, :]
+        rows = jnp.concatenate([rows[first:], rows[:first]], axis=0)
         ordered = jnp.dot(place, rows, preferred_element_type=F32).astype(BF16)
-        out_ref[0, :, part * LANES : (part + 1) * LANES] = ordered
+        out_ref[0, :, part * lanes : (part + 1) * lanes] = ordered
 
 
 def per_device(codes, row_scales, history_lengths, history_ids, query_items, slot_tables):
@@ -254,7 +253,7 @@
 
     along_x = [[device(t, y, x) for x in x_order] for t in tables for y in ys]
     along_y = [[device(t, y, x) for y in y_order] for t in tables for x in xs]
-    to_owner = [[device(t, y, x) for y in y_order for t in tbl_order] for x in xs]
+    along_tbl = [[device(t, y, x) for t in tbl_order] for y in ys for x in xs]
 
     def exchange(blocks, groups):
         return lax.all_to_all(
@@ -275,14 +274,15 @@
     )(codes[0], row_scales)
     table = exchange(packed, along_x)
     grp = lax.axis_index("grp").astype(jnp.int32).reshape(1)
-    counts, target = pl.pallas_call(
+    counts, target, place = pl.pallas_call(
         functools.partial(count_kernel, order),
         out_shape=[
             jax.ShapeDtypeStruct((samples, held), F32),
             jax.ShapeDtypeStruct((samples, held), F32),
+            jax.ShapeDtypeStruct((tbl_count, tbl_count), F32),
         ],
-        in_specs=[SMEM, VMEM, VMEM, VMEM],
-        out_specs=[VMEM, VMEM],
+        in_specs=[SMEM, VMEM, VMEM, VMEM, VMEM],
+        out_specs=[VMEM, VMEM, VMEM],
         scratch_shapes=[
             pltpu.VMEM((samples, history), jnp.int32),
             pltpu.VMEM((samples, LANES), jnp.int32),
@@ -290,7 +290,13 @@
         cost_estimate=pl.CostEstimate(flops=100_000_000, bytes_accessed=1_000_000, transcendentals=0),
         compiler_params=SMALL,
         name="count",
-    )(grp, history_ids[:, 0, :].T, history_lengths.T, query_items.T)
+    )(
+        grp,
+        history_ids[:, 0, :].T,
+        history_lengths.T,
+        query_items.T,
+        slot_tables.reshape(1, tbl_count),
+    )
     masked = pl.pallas_call(
         query_kernel,
         out_shape=jax.ShapeDtypeStruct((y_count, samples + SCALE_ROWS, width), BF16),
@@ -302,22 +308,31 @@
     query = exchange(masked, along_y)
     partial = pl.pallas_call(
         pool_kernel,
-        out_shape=jax.ShapeDtypeStruct((samples, 2 * (width // LANES), LANES), BF16),
+        out_shape=jax.ShapeDtypeStruct((y_count, samples // y_count, width + LANES), F32),
         in_specs=[VMEM, VMEM, VMEM],
         out_specs=VMEM,
         scratch_shapes=[pltpu.VMEM((samples, held), F32)],
         compiler_params=SMALL,
         name="pool",
     )(table, counts, query)
-    got = exchange(partial, to_owner)
+    got = exchange(partial, along_y)
+    pooled = pl.pallas_call(
+        merge_kernel,
+        out_shape=jax.ShapeDtypeStruct((tbl_count, width // LANES, LANES), BF16),
+        in_specs=[VMEM],
+        out_specs=VMEM,
+        compiler_params=SMALL,
+        name="merge",
+    )(got)
+    arrived = exchange(pooled, along_tbl)
     return pl.pallas_call(
-        functools.partial(combine_kernel, order),
+        functools.partial(order_kernel, tbl_order),
         out_shape=jax.ShapeDtypeStruct((1, tbl_count, width), BF16),
         in_specs=[VMEM, VMEM],
         out_specs=VMEM,
         compiler_params=SMALL,
-        name="combine",
-    )(slot_tables.reshape(1, tbl_count), got)
+        name="order",
+    )(place, arrived)
 
 
 def solution(mesh):

time: 59.2 us -> 57.9 us (0.978)
  Pallas kernels: 8.22 us -> 7.48 us
  local copies, waits for them, and re-layouts: 1.34 us -> 0.69 us
    pallas_call x2 -> x3, Pallas kernels: 2.63 us -> 1.89 us  [the longest x1 0.93 us: per_device(): pl.pallas_call(pool_kernel, out_shape=jax.ShapeDtypeStruct((y_count, samp...]
    unnamed x8, local copies, waits for them, and re-layouts: 1.34 us -> 0.69 us
    all_to_all x2 -> x3, blocking collectives: 42 us -> 42.1 us  [exchange(): lax.all_to_all(blocks, ('tbl', 'grp'), 0, 0, axis_index_groups=groups, ti...]
where the time goes in v4:
time: 57.9 us; the launch traced here: 57.6 us
  blocking collectives  42.1 us (73%)
  Pallas kernels  7.48 us (13%)
  starting transfers between devices  7.15 us (12%)
  local copies, waits for them, and re-layouts  0.69 us (1%)
    all_to_all x3, blocking collectives, exchange(): lax.all_to_all(blocks, ('tbl', 'grp'), 0, 0, axis_index_groups=groups, ti...  42.1 us
    all_to_all x1, starting transfers between devices, exchange(): lax.all_to_all(blocks, ('tbl', 'grp'), 0, 0, axis_index_groups=groups, ti...  7.15 us
    pallas_call x1, Pallas kernels, per_device(): pl.pallas_call(functools.partial(count_kernel, order), out_shape=[jax.Sha...  3.54 us
    pallas_call x1, Pallas kernels, per_device(): pl.pallas_call(pack_kernel, out_shape=jax.ShapeDtypeStruct((x_count, rows...  1.76 us
  transfers between devices with their start and end apart: 1, of which 1 were waited for; matrix products, arithmetic and copies ran while one was open for 0% of the time, Pallas kernels for 6%

profile of v4, /device:TPU:1, one launch (start us, length us, event | category | flops | bytes accessed | tf_op | source)
XLA Modules:
  0.0 57.6 jit_solution(8530670051633801911)
XLA Ops:
  0.0 1.8 %pack.1 = bf16[4,264,256]{2,1,0:T(8,128)(2,1)} custom-call(bf16[256,256]{1,0:T(8,128)(2,1)} %bitcast.12, f32[1,256]{1,0:T(1,128)} %scales_ref.1), custom_call_target="tpu_custom_call" | custom-call | tf_op jit(solution)/shard_map/pack/pallas_call | solution.py:263
  1.8 0.0 copy-start
  1.8 0.0 copy-start.2
  1.8 7.1 %all-to-all-start = ((bf16[4,264,256]{2,1,0:T(8,128)(2,1)}), bf16[4,264,256]{2,1,0:T(8,128)(2,1)S(1)}, u32[]{:S(2)}, u32[]{:S(2)}) async-start(bf16[4,264,256]{2,1,0:T(8,128)(2,1)} %pack.1), calls=%async_computation | async-start | bytes 1081344 | tf_op jit(solution)/shard_map/all_to_all | solution.py:259
  8.9 0.0 copy-start.1
  8.9 0.0 copy-start.3
  8.9 0.0 copy-done
  8.9 0.0 copy-done.2
  8.9 0.7 %copy-done.1 = s32[512,1]{0,1:T(1,128)S(1)} copy-done((s32[512,1]{0,1:T(1,128)S(1)}, s32[512,1]{0,1:T(1,128)}, u32[]{:S(2)}) %copy-start.1) | copy-done | bytes 2072
  9.6 0.0 copy-done.3
  9.6 3.5 %count.1 = (f32[128,1024]{1,0:T(8,128)S(1)}, f32[128,1024]{1,0:T(8,128)S(1)}, f32[32,32]{1,0:T(8,128)S(1)}) custom-call(s32[1]{0:T(128)} %bitcast.grp_ref, s32[32,512]{1,0:T(8,128)S(1)} %bitcast.8, s32[1,512]{1,0:T(1,128)S(1)} %bitcast.9, s32[1,512]{1,0:T(1,128)S(1)} %bitcast.10, s32[1,32]{1,0:T(1,128)S(1)} %bitcast.11), custom_call_target="tpu_custom_call" | custom-call | flops 100000000 | bytes 1000000 | tf_op jit(solution)/shard_map/count/pallas_call | solution.py:277
  13.2 0.1 all-to-all-done.table_ref
  13.3 0.3 query.1
  13.6 10.3 %all_to_all.20.query_ref = bf16[4,136,256]{2,1,0:T(8,128)(2,1)S(1)} all-to-all(bf16[4,136,256]{2,1,0:T(8,128)(2,1)S(1)} %query.1), channel_id=1, replica_groups={{8,12,0,4},{9,13,1,5},{10,14,2,6},{11,15,3,7},{24,28,16,20},{25,29,17,2..., dimensions={0} | all-to-all | bytes 557056 | tf_op jit(solution)/shard_map/all_to_all | solution.py:259
  23.9 0.9 %pool.1 = f32[4,32,384]{2,1,0:T(8,128)S(1)} custom-call(bf16[4,264,256]{2,1,0:T(8,128)(2,1)S(1)} %all-to-all-done.table_ref, f32[128,1024]{1,0:T(8,128)S(1)} %get-tuple-element.9.counts_ref, bf16[4,136,256]{2,1,0:T(8,128)(2,1)S(1)} %all_to_all.20.query_ref), custom_call_target="tpu_custom_call" | custom-call | tf_op jit(solution)/shard_map/pool/pallas_call | solution.py:309
  24.8 7.6 %all_to_all.21.got_ref = f32[4,32,384]{2,1,0:T(8,128)S(1)} all-to-all(f32[4,32,384]{2,1,0:T(8,128)S(1)} %pool.1), channel_id=1, replica_groups={{8,12,0,4},{9,13,1,5},{10,14,2,6},{11,15,3,7},{24,28,16,20},{25,29,17,2..., dimensions={0} | all-to-all | bytes 393216 | tf_op jit(solution)/shard_map/all_to_all | solution.py:259
  32.5 0.2 merge.1
  32.7 24.1 %all_to_all.22.pooled_ref = bf16[32,2,128]{2,1,0:T(2,128)(2,1)S(1)} all-to-all(bf16[32,2,128]{2,1,0:T(2,128)(2,1)S(1)} %merge.1), channel_id=1, replica_groups={{256,272,288,304,320,336,352,368,384,400,416,432,448,464,480,496,0,16,3..., dimensions={0} | all-to-all | bytes 32768 | tf_op jit(solution)/shard_map/all_to_all | solution.py:259
  56.8 0.8 %order.1 = bf16[1,32,256]{2,1,0:T(8,128)(2,1)} custom-call(f32[32,32]{1,0:T(8,128)S(1)} %get-tuple-element.8.place_ref, bf16[32,2,128]{2,1,0:T(2,128)(2,1)S(1)} %all_to_all.22.pooled_ref), custom_call_target="tpu_custom_call" | custom-call | tf_op jit(solution)/shard_map/order/pallas_call | solution.py:328
Async XLA Ops:
  1.8 7.2 %copy-start = (s32[512,1,32]{0,2,1:T(8,128)S(1)}, s32[512,1,32]{0,2,1:T(8,128)}, u32[]{:S(2)}) copy-start(s32[512,1,32]{0,2,1:T(8,128)} %param.9) | copy-start | bytes 196612
  1.8 7.2 %copy-start.2 = (s32[512,1]{0,1:T(1,128)S(1)}, s32[512,1]{0,1:T(1,128)}, u32[]{:S(2)}) copy-start(s32[512,1]{0,1:T(1,128)} %param.10) | copy-start | bytes 6148
  1.8 11.5 %all-to-all-start = ((bf16[4,264,256]{2,1,0:T(8,128)(2,1)}), bf16[4,264,256]{2,1,0:T(8,128)(2,1)S(1)}, u32[]{:S(2)}, u32[]{:S(2)}) async-start(bf16[4,264,256]{2,1,0:T(8,128)(2,1)} %pack.1), calls=%async_computation | async-start | bytes 1081344 | tf_op jit(solution)/shard_map/all_to_all | solution.py:259
  8.9 0.7 %copy-start.1 = (s32[512,1]{0,1:T(1,128)S(1)}, s32[512,1]{0,1:T(1,128)}, u32[]{:S(2)}) copy-start(s32[512,1]{0,1:T(1,128)} %param.8) | copy-start | bytes 6148
  8.9 0.7 %copy-start.3 = (s32[32]{0:T(128)S(1)}, s32[32]{0:T(128)}, u32[]{:S(2)}) copy-start(s32[32]{0:T(128)} %param.11) | copy-start | bytes 388

commit v5 on v4

--- a/solution.py
+++ b/solution.py
@@ -15,7 +15,7 @@
 SMALL = pltpu.CompilerParams(vmem_limit_bytes=16 << 20)
 SCALE_ROWS = 8
 LANES = 128
-CHIPS_X = 4
+CHIPS_SIDE = 4
 
 
 def rotated(count, first):
@@ -56,6 +56,7 @@
 
 def count_kernel(
     order,
+    tbl_ref,
     grp_ref,
     ids_ref,
     lengths_ref,
@@ -67,14 +68,18 @@
     names_ref,
     item_ref,
 ):
-    tbl_order, y_order, x_order = order
+    tbl_order, side_order = order
     history, batch = ids_ref.shape
     samples, held = counts_ref.shape
-    tbl_count, x_count = len(tbl_order), len(x_order)
-    grp_count = batch // tbl_count
-    rows = held // x_count
-    grp = grp_ref[0]
-    y, x = grp // x_count, grp % x_count
+    tbl_count, side = len(tbl_order), len(side_order)
+    rows = held // side
+    turned = tbl_ref[0] % 2 == 1
+
+    def split(grp):
+        y, x = grp // side, grp % side
+        return jnp.where(turned, y, x), jnp.where(turned, x, y)
+
+    along, across = split(grp_ref[0])
     ids = ids_ref[...]
     items = items_ref[...]
     extra = jnp.concatenate(
@@ -93,15 +98,16 @@
     sample = lax.broadcasted_iota(jnp.int32, (samples, batch), 0)
     column = lax.broadcasted_iota(jnp.int32, (samples, batch), 1)
     tbl_at = (sample % tbl_count + tbl_order[0]) % tbl_count
-    y_at = (sample // tbl_count + y_order[0]) % len(y_order)
-    chosen = jnp.where(column == tbl_at * grp_count + y_at * x_count + x, 1.0, 0.0).astype(BF16)
+    across_at = (sample // tbl_count + side_order[0]) % side
+    grp_at = jnp.where(turned, along * side + across_at, across_at * side + along)
+    chosen = jnp.where(column == tbl_at * side * side + grp_at, 1.0, 0.0).astype(BF16)
     own = lax.dot_general(chosen, digits, (((1,), (1,)), ((), ())), preferred_element_type=F32)
 
     def held_at(high, low):
         row = (high * 64.0 + low).astype(jnp.int32)
-        owner = row // rows
-        block = (owner % x_count - x_order[0] + x_count) % x_count
-        return jnp.where(owner // x_count == y, block * rows + row % rows, -1)
+        owner_along, owner_across = split(row // rows)
+        block = (owner_along - side_order[0] + side) % side
+        return jnp.where(owner_across == across, block * rows + row % rows, -1)
 
     own_lengths = own[:, 2 * history : 2 * history + 1].astype(jnp.int32)
     position = lax.broadcasted_iota(jnp.int32, (samples, history), 1)
@@ -238,22 +244,21 @@
     batch, _, history = history_ids.shape
     tbl_count = lax.axis_size("tbl")
     grp_count = lax.axis_size("grp")
-    x_count = CHIPS_X
-    y_count = grp_count // x_count
-    samples = batch // x_count
-    held = rows * x_count
-    tbl_order = rotated(tbl_count, tbl_count // 2)
-    y_order = rotated(y_count, y_count // 2)
-    x_order = rotated(x_count, x_count // 2)
-    order = (tbl_order, y_order, x_order)
-    tables, ys, xs = range(tbl_count), range(y_count), range(x_count)
-
-    def device(t, y, x):
-        return (t * y_count + y) * x_count + x
-
-    along_x = [[device(t, y, x) for x in x_order] for t in tables for y in ys]
-    along_y = [[device(t, y, x) for y in y_order] for t in tables for x in xs]
-    along_tbl = [[device(t, y, x) for t in tbl_order] for y in ys for x in xs]
+    side = CHIPS_SIDE
+    samples = tbl_count * side
+    held = rows * side
+    tbl_order = rotated(tbl_count, tbl_count // 2 + 1)
+    side_order = rotated(side, side // 2)
+    order = (tbl_order, side_order)
+    tables, places = range(tbl_count), range(side)
+
+    def device(t, along, across):
+        y, x = (along, across) if t % 2 else (across, along)
+        return (t * side + y) * side + x
+
+    along_rows = [[device(t, u, v) for u in side_order] for t in tables for v in places]
+    across_rows = [[device(t, u, v) for v in side_order] for t in tables for u in places]
+    along_tbl = [[t * grp_count + g for t in tbl_order] for g in range(grp_count)]
 
     def exchange(blocks, groups):
         return lax.all_to_all(
@@ -262,17 +267,18 @@
 
     packed = pl.pallas_call(
         pack_kernel,
-        out_shape=jax.ShapeDtypeStruct((x_count, rows + SCALE_ROWS, width), BF16),
+        out_shape=jax.ShapeDtypeStruct((side, rows + SCALE_ROWS, width), BF16),
         in_specs=[HBM, HBM],
         out_specs=HBM,
         scratch_shapes=[
             pltpu.VMEM((rows + SCALE_ROWS, width), BF16),
             pltpu.VMEM((1, rows), F32),
-            pltpu.SemaphoreType.DMA((x_count + 2,)),
+            pltpu.SemaphoreType.DMA((side + 2,)),
         ],
         name="pack",
     )(codes[0], row_scales)
-    table = exchange(packed, along_x)
+    table = exchange(packed, along_rows)
+    tbl = lax.axis_index("tbl").astype(jnp.int32).reshape(1)
     grp = lax.axis_index("grp").astype(jnp.int32).reshape(1)
     counts, target, place = pl.pallas_call(
         functools.partial(count_kernel, order),
@@ -281,7 +287,7 @@
             jax.ShapeDtypeStruct((samples, held), F32),
             jax.ShapeDtypeStruct((tbl_count, tbl_count), F32),
         ],
-        in_specs=[SMEM, VMEM, VMEM, VMEM, VMEM],
+        in_specs=[SMEM, SMEM, VMEM, VMEM, VMEM, VMEM],
         out_specs=[VMEM, VMEM, VMEM],
         scratch_shapes=[
             pltpu.VMEM((samples, history), jnp.int32),
@@ -291,6 +297,7 @@
         compiler_params=SMALL,
         name="count",
     )(
+        tbl,
         grp,
         history_ids[:, 0, :].T,
         history_lengths.T,
@@ -299,23 +306,23 @@
     )
     masked = pl.pallas_call(
         query_kernel,
-        out_shape=jax.ShapeDtypeStruct((y_count, samples + SCALE_ROWS, width), BF16),
+        out_shape=jax.ShapeDtypeStruct((side, samples + SCALE_ROWS, width), BF16),
         in_specs=[VMEM, VMEM],
         out_specs=VMEM,
         compiler_params=SMALL,
         name="query",
     )(table, target)
-    query = exchange(masked, along_y)
+    query = exchange(masked, across_rows)
     partial = pl.pallas_call(
         pool_kernel,
-        out_shape=jax.ShapeDtypeStruct((y_count, samples // y_count, width + LANES), F32),
+        out_shape=jax.ShapeDtypeStruct((side, samples // side, width + LANES), F32),
         in_specs=[VMEM, VMEM, VMEM],
         out_specs=VMEM,
         scratch_shapes=[pltpu.VMEM((samples, held), F32)],
         compiler_params=SMALL,
         name="pool",
     )(table, counts, query)
-    got = exchange(partial, along_y)
+    got = exchange(partial, across_rows)
     pooled = pl.pallas_call(
         merge_kernel,
         out_shape=jax.ShapeDtypeStruct((tbl_count, width // LANES, LANES), BF16),

time: 57.9 us -> 55.8 us (0.964)
  blocking collectives: 42.1 us -> 39.9 us
    all_to_all x3, blocking collectives: 42.1 us -> 39.9 us  [exchange(): lax.all_to_all(blocks, ('tbl', 'grp'), 0, 0, axis_index_groups=groups, ti...]
where the time goes in v5:
time: 55.8 us; the launch traced here: 55.5 us
  blocking collectives  39.9 us (72%)
  Pallas kernels  7.5 us (13%)
  starting transfers between devices  7.32 us (13%)
  local copies, waits for them, and re-layouts  0.7 us (1%)
    all_to_all x3, blocking collectives, exchange(): lax.all_to_all(blocks, ('tbl', 'grp'), 0, 0, axis_index_groups=groups, ti...  39.9 us
    all_to_all x1, starting transfers between devices, exchange(): lax.all_to_all(blocks, ('tbl', 'grp'), 0, 0, axis_index_groups=groups, ti...  7.32 us
    pallas_call x1, Pallas kernels, per_device(): pl.pallas_call(functools.partial(count_kernel, order), out_shape=[jax.Sha...  3.55 us
    pallas_call x1, Pallas kernels, per_device(): pl.pallas_call(pack_kernel, out_shape=jax.ShapeDtypeStruct((side, rows +...  1.76 us
  transfers between devices with their start and end apart: 1, of which 1 were waited for; matrix products, arithmetic and copies ran while one was open for 0% of the time, Pallas kernels for 6%

profile of v5, /device:TPU:1, one launch (start us, length us, event | category | flops | bytes accessed | tf_op | source)
XLA Modules:
  0.0 55.5 jit_solution(16459945151224853551)
XLA Ops:
  0.0 1.8 %pack.1 = bf16[4,264,256]{2,1,0:T(8,128)(2,1)} custom-call(bf16[256,256]{1,0:T(8,128)(2,1)} %bitcast.13, f32[1,256]{1,0:T(1,128)} %scales_ref.1), custom_call_target="tpu_custom_call" | custom-call | tf_op jit(solution)/shard_map/pack/pallas_call | solution.py:268
  1.8 0.0 copy-start
  1.8 7.3 %all-to-all-start = ((bf16[4,264,256]{2,1,0:T(8,128)(2,1)}), bf16[4,264,256]{2,1,0:T(8,128)(2,1)S(1)}, u32[]{:S(2)}, u32[]{:S(2)}) async-start(bf16[4,264,256]{2,1,0:T(8,128)(2,1)} %pack.1), calls=%async_computation | async-start | bytes 1081344 | tf_op jit(solution)/shard_map/all_to_all | solution.py:264
  9.1 0.0 copy-start.2
  9.1 0.0 copy-start.1
  9.1 0.0 copy-start.3
  9.1 0.0 copy-done
  9.1 0.7 %copy-done.2 = s32[512,1]{0,1:T(1,128)S(1)} copy-done((s32[512,1]{0,1:T(1,128)S(1)}, s32[512,1]{0,1:T(1,128)}, u32[]{:S(2)}) %copy-start.2) | copy-done | bytes 2072
  9.8 0.0 copy-done.1
  9.8 0.0 copy-done.3
  9.8 3.5 %count.1 = (f32[128,1024]{1,0:T(8,128)S(1)}, f32[128,1024]{1,0:T(8,128)S(1)}, f32[32,32]{1,0:T(8,128)S(1)}) custom-call(s32[1]{0:T(128)} %bitcast.tbl_ref, s32[1]{0:T(128)} %bitcast.1.grp_ref, s32[32,512]{1,0:T(8,128)S(1)} %bitcast.9, s32[1,512]{1,0:T(1,128)S(1)} %bitcast.10, s32[1,512]{1,0:T(1,128)S(1)} %bitcast.11, s32[1,32]{1,0:T(1,128)S(1)} %bitcast.12), custom_call_target="tpu_custom_call" | custom-call | flops 100000000 | bytes 1000000 | tf_op jit(solution)/shard_map/count/pallas_call | solution.py:283
  13.4 0.1 all-to-all-done.table_ref
  13.4 0.3 query.1
  13.7 8.0 %all_to_all.20.query_ref = bf16[4,136,256]{2,1,0:T(8,128)(2,1)S(1)} all-to-all(bf16[4,136,256]{2,1,0:T(8,128)(2,1)S(1)} %query.1), channel_id=1, replica_groups={{8,12,0,4},{9,13,1,5},{10,14,2,6},{11,15,3,7},{18,19,16,17},{22,23,20,2..., dimensions={0} | all-to-all | bytes 557056 | tf_op jit(solution)/shard_map/all_to_all | solution.py:264
  21.8 0.9 %pool.1 = f32[4,32,384]{2,1,0:T(8,128)S(1)} custom-call(bf16[4,264,256]{2,1,0:T(8,128)(2,1)S(1)} %all-to-all-done.table_ref, f32[128,1024]{1,0:T(8,128)S(1)} %get-tuple-element.9.counts_ref, bf16[4,136,256]{2,1,0:T(8,128)(2,1)S(1)} %all_to_all.20.query_ref), custom_call_target="tpu_custom_call" | custom-call | tf_op jit(solution)/shard_map/pool/pallas_call | solution.py:316
  22.7 7.5 %all_to_all.21.got_ref = f32[4,32,384]{2,1,0:T(8,128)S(1)} all-to-all(f32[4,32,384]{2,1,0:T(8,128)S(1)} %pool.1), channel_id=1, replica_groups={{8,12,0,4},{9,13,1,5},{10,14,2,6},{11,15,3,7},{18,19,16,17},{22,23,20,2..., dimensions={0} | all-to-all | bytes 393216 | tf_op jit(solution)/shard_map/all_to_all | solution.py:264
  30.2 0.2 merge.1
  30.4 24.3 %all_to_all.22.pooled_ref = bf16[32,2,128]{2,1,0:T(2,128)(2,1)S(1)} all-to-all(bf16[32,2,128]{2,1,0:T(2,128)(2,1)S(1)} %merge.1), channel_id=1, replica_groups={{272,288,304,320,336,352,368,384,400,416,432,448,464,480,496,0,16,32,48..., dimensions={0} | all-to-all | bytes 32768 | tf_op jit(solution)/shard_map/all_to_all | solution.py:264
  54.7 0.8 %order.1 = bf16[1,32,256]{2,1,0:T(8,128)(2,1)} custom-call(f32[32,32]{1,0:T(8,128)S(1)} %get-tuple-element.8.place_ref, bf16[32,2,128]{2,1,0:T(2,128)(2,1)S(1)} %all_to_all.22.pooled_ref), custom_call_target="tpu_custom_call" | custom-call | tf_op jit(solution)/shard_map/order/pallas_call | solution.py:335
Async XLA Ops:
  1.8 7.3 %copy-start = (s32[512,1,32]{0,2,1:T(8,128)S(1)}, s32[512,1,32]{0,2,1:T(8,128)}, u32[]{:S(2)}) copy-start(s32[512,1,32]{0,2,1:T(8,128)} %param.9) | copy-start | bytes 196612
  1.8 11.7 %all-to-all-start = ((bf16[4,264,256]{2,1,0:T(8,128)(2,1)}), bf16[4,264,256]{2,1,0:T(8,128)(2,1)S(1)}, u32[]{:S(2)}, u32[]{:S(2)}) async-start(bf16[4,264,256]{2,1,0:T(8,128)(2,1)} %pack.1), calls=%async_computation | async-start | bytes 1081344 | tf_op jit(solution)/shard_map/all_to_all | solution.py:264
  9.1 0.7 %copy-start.2 = (s32[512,1]{0,1:T(1,128)S(1)}, s32[512,1]{0,1:T(1,128)}, u32[]{:S(2)}) copy-start(s32[512,1]{0,1:T(1,128)} %param.10) | copy-start | bytes 6148
  9.1 0.7 %copy-start.1 = (s32[512,1]{0,1:T(1,128)S(1)}, s32[512,1]{0,1:T(1,128)}, u32[]{:S(2)}) copy-start(s32[512,1]{0,1:T(1,128)} %param.8) | copy-start | bytes 6148
  9.1 0.7 %copy-start.3 = (s32[32]{0:T(128)S(1)}, s32[32]{0:T(128)}, u32[]{:S(2)}) copy-start(s32[32]{0:T(128)} %param.11) | copy-start | bytes 388

commit v6 on v5

--- a/solution.py
+++ b/solution.py
@@ -73,7 +73,7 @@
     samples, held = counts_ref.shape
     tbl_count, side = len(tbl_order), len(side_order)
     rows = held // side
-    turned = tbl_ref[0] % 2 == 1
+    turned = tbl_ref[0] % 2 == 0
 
     def split(grp):
         y, x = grp // side, grp % side
@@ -117,23 +117,28 @@
         own[:, 2 * history + 1 : 2 * history + 2], own[:, 2 * history + 2 : 2 * history + 3]
     )
     item_ref[...] = jnp.broadcast_to(item, item_ref.shape)
-    lane = lax.broadcasted_iota(jnp.int32, (8, LANES), 1)
+    lane = lax.broadcasted_iota(jnp.int32, (16, LANES), 1)
+    one = jnp.ones((16, LANES), BF16)
+    none = jnp.zeros((16, LANES), BF16)
 
     def group(k, carry):
-        at = pl.ds(pl.multiple_of(k * 8, 8), 8)
+        at = pl.ds(pl.multiple_of(k * 16, 16), 16)
         named = names_ref[at, :]
-        named = [jnp.broadcast_to(named[:, h : h + 1], (8, LANES)) for h in range(history)]
+        named = [
+            jnp.broadcast_to(named[:, h : h + 1], (16, LANES)).astype(jnp.int16)
+            for h in range(history)
+        ]
         item = item_ref[at, :]
         for first in range(0, held, LANES):
-            row = lane + first
-            total = jnp.zeros((8, LANES), F32)
+            row = (lane + first).astype(jnp.int16)
+            total = none
             for h in range(history):
-                total = total + jnp.where(named[h] == row, 1.0, 0.0)
-            counts_ref[at, first : first + LANES] = total
-            target_ref[at, first : first + LANES] = jnp.where(item == row, 1.0, 0.0)
+                total = total + jnp.where(named[h] == row, one, none)
+            counts_ref[at, first : first + LANES] = total.astype(F32)
+            target_ref[at, first : first + LANES] = jnp.where(item == lane + first, 1.0, 0.0)
         return carry
 
-    lax.fori_loop(0, samples // 8, group, 0)
+    lax.fori_loop(0, samples // 16, group, 0)
     table = lax.broadcasted_iota(jnp.int32, place_ref.shape, 0)
     place_ref[...] = jnp.where(table == tables_ref[...], 1.0, 0.0)
 
@@ -247,13 +252,13 @@
     side = CHIPS_SIDE
     samples = tbl_count * side
     held = rows * side
-    tbl_order = rotated(tbl_count, tbl_count // 2 + 1)
+    tbl_order = rotated(tbl_count, tbl_count // 2 + 3)
     side_order = rotated(side, side // 2)
     order = (tbl_order, side_order)
     tables, places = range(tbl_count), range(side)
 
     def device(t, along, across):
-        y, x = (along, across) if t % 2 else (across, along)
+        y, x = (across, along) if t % 2 else (along, across)
         return (t * side + y) * side + x
 
     along_rows = [[device(t, u, v) for u in side_order] for t in tables for v in places]

time: 55.8 us -> 55.8 us (level)
  Pallas kernels: 7.5 us -> 6.06 us
  waiting for transfers between devices: 0.08 us -> 1.51 us
    pallas_call x1, Pallas kernels: 3.55 us -> 2.11 us  [per_device(): pl.pallas_call(functools.partial(count_kernel, order), out_shape=[jax.Sha...]
    all_to_all x1, waiting for transfers between devices: 0.08 us -> 1.51 us  [exchange(): lax.all_to_all(blocks, ('tbl', 'grp'), 0, 0, axis_index_groups=groups, ti...]
  transfers between devices with their start and end apart: 1 -> 1, of which waited for: 1 -> 1; matrix products, arithmetic and copies ran while one was open for 0% -> 0% of each run, Pallas kernels for 6% -> 4%
where the time goes in v6:
time: 55.8 us; the launch traced here: 55.5 us
  blocking collectives  40 us (72%)
  starting transfers between devices  7.15 us (13%)
  Pallas kernels  6.06 us (11%)
  waiting for transfers between devices  1.51 us (3%)
  local copies, waits for them, and re-layouts  0.7 us (1%)
    all_to_all x3, blocking collectives, exchange(): lax.all_to_all(blocks, ('tbl', 'grp'), 0, 0, axis_index_groups=groups, ti...  40 us
    all_to_all x1, starting transfers between devices, exchange(): lax.all_to_all(blocks, ('tbl', 'grp'), 0, 0, axis_index_groups=groups, ti...  7.15 us
    pallas_call x1, Pallas kernels, per_device(): pl.pallas_call(functools.partial(count_kernel, order), out_shape=[jax.Sha...  2.11 us
    pallas_call x1, Pallas kernels, per_device(): pl.pallas_call(pack_kernel, out_shape=jax.ShapeDtypeStruct((side, rows +...  1.76 us
    all_to_all x1, waiting for transfers between devices, exchange(): lax.all_to_all(blocks, ('tbl', 'grp'), 0, 0, axis_index_groups=groups, ti...  1.51 us
  transfers between devices with their start and end apart: 1, of which 1 were waited for; matrix products, arithmetic and copies ran while one was open for 0% of the time, Pallas kernels for 4%

profile of v6, /device:TPU:1, one launch (start us, length us, event | category | flops | bytes accessed | tf_op | source)
XLA Modules:
  0.0 55.5 jit_solution(5930146555189760165)
XLA Ops:
  0.0 1.8 %pack.1 = bf16[4,264,256]{2,1,0:T(8,128)(2,1)} custom-call(bf16[256,256]{1,0:T(8,128)(2,1)} %bitcast.13, f32[1,256]{1,0:T(1,128)} %scales_ref.1), custom_call_target="tpu_custom_call" | custom-call | tf_op jit(solution)/shard_map/pack/pallas_call | solution.py:273
  1.8 0.0 copy-start
  1.8 7.1 %all-to-all-start = ((bf16[4,264,256]{2,1,0:T(8,128)(2,1)}), bf16[4,264,256]{2,1,0:T(8,128)(2,1)S(1)}, u32[]{:S(2)}, u32[]{:S(2)}) async-start(bf16[4,264,256]{2,1,0:T(8,128)(2,1)} %pack.1), calls=%async_computation | async-start | bytes 1081344 | tf_op jit(solution)/shard_map/all_to_all | solution.py:269
  8.9 0.0 copy-start.2
  8.9 0.0 copy-start.1
  8.9 0.0 copy-start.3
  8.9 0.0 copy-done
  8.9 0.7 %copy-done.2 = s32[512,1]{0,1:T(1,128)S(1)} copy-done((s32[512,1]{0,1:T(1,128)S(1)}, s32[512,1]{0,1:T(1,128)}, u32[]{:S(2)}) %copy-start.2) | copy-done | bytes 2072
  9.6 0.0 copy-done.1
  9.6 0.0 copy-done.3
  9.6 2.1 %count.1 = (f32[128,1024]{1,0:T(8,128)S(1)}, f32[128,1024]{1,0:T(8,128)S(1)}, f32[32,32]{1,0:T(8,128)S(1)}) custom-call(s32[1]{0:T(128)} %bitcast.tbl_ref, s32[1]{0:T(128)} %bitcast.1.grp_ref, s32[32,512]{1,0:T(8,128)S(1)} %bitcast.9, s32[1,512]{1,0:T(1,128)S(1)} %bitcast.10, s32[1,512]{1,0:T(1,128)S(1)} %bitcast.11, s32[1,32]{1,0:T(1,128)S(1)} %bitcast.12), custom_call_target="tpu_custom_call" | custom-call | flops 100000000 | bytes 1000000 | tf_op jit(solution)/shard_map/count/pallas_call | solution.py:288
  11.7 1.5 %all-to-all-done.table_ref = bf16[4,264,256]{2,1,0:T(8,128)(2,1)S(1)} async-done(((bf16[4,264,256]{2,1,0:T(8,128)(2,1)}), bf16[4,264,256]{2,1,0:T(8,128)(2,1)S(1)}, u32[]{:S(2)}, u32[]{:S(2)}) %all-to-all-start) | async-done | bytes 540704 | tf_op jit(solution)/shard_map/all_to_all | solution.py:269
  13.3 0.3 query.1
  13.6 8.2 %all_to_all.20.query_ref = bf16[4,136,256]{2,1,0:T(8,128)(2,1)S(1)} all-to-all(bf16[4,136,256]{2,1,0:T(8,128)(2,1)S(1)} %query.1), channel_id=1, replica_groups={{2,3,0,1},{6,7,4,5},{10,11,8,9},{14,15,12,13},{24,28,16,20},{25,29,17,2..., dimensions={0} | all-to-all | bytes 557056 | tf_op jit(solution)/shard_map/all_to_all | solution.py:269
  21.8 0.9 %pool.1 = f32[4,32,384]{2,1,0:T(8,128)S(1)} custom-call(bf16[4,264,256]{2,1,0:T(8,128)(2,1)S(1)} %all-to-all-done.table_ref, f32[128,1024]{1,0:T(8,128)S(1)} %get-tuple-element.9.counts_ref, bf16[4,136,256]{2,1,0:T(8,128)(2,1)S(1)} %all_to_all.20.query_ref), custom_call_target="tpu_custom_call" | custom-call | tf_op jit(solution)/shard_map/pool/pallas_call | solution.py:321
  22.7 7.5 %all_to_all.21.got_ref = f32[4,32,384]{2,1,0:T(8,128)S(1)} all-to-all(f32[4,32,384]{2,1,0:T(8,128)S(1)} %pool.1), channel_id=1, replica_groups={{2,3,0,1},{6,7,4,5},{10,11,8,9},{14,15,12,13},{24,28,16,20},{25,29,17,2..., dimensions={0} | all-to-all | bytes 393216 | tf_op jit(solution)/shard_map/all_to_all | solution.py:269
  30.2 0.2 merge.1
  30.4 24.2 %all_to_all.22.pooled_ref = bf16[32,2,128]{2,1,0:T(2,128)(2,1)S(1)} all-to-all(bf16[32,2,128]{2,1,0:T(2,128)(2,1)S(1)} %merge.1), channel_id=1, replica_groups={{304,320,336,352,368,384,400,416,432,448,464,480,496,0,16,32,48,64,80,9..., dimensions={0} | all-to-all | bytes 32768 | tf_op jit(solution)/shard_map/all_to_all | solution.py:269
  54.7 0.8 %order.1 = bf16[1,32,256]{2,1,0:T(8,128)(2,1)} custom-call(f32[32,32]{1,0:T(8,128)S(1)} %get-tuple-element.8.place_ref, bf16[32,2,128]{2,1,0:T(2,128)(2,1)S(1)} %all_to_all.22.pooled_ref), custom_call_target="tpu_custom_call" | custom-call | tf_op jit(solution)/shard_map/order/pallas_call | solution.py:340
Async XLA Ops:
  1.8 7.2 %copy-start = (s32[512,1,32]{0,2,1:T(8,128)S(1)}, s32[512,1,32]{0,2,1:T(8,128)}, u32[]{:S(2)}) copy-start(s32[512,1,32]{0,2,1:T(8,128)} %param.9) | copy-start | bytes 196612
  1.8 11.5 %all-to-all-start = ((bf16[4,264,256]{2,1,0:T(8,128)(2,1)}), bf16[4,264,256]{2,1,0:T(8,128)(2,1)S(1)}, u32[]{:S(2)}, u32[]{:S(2)}) async-start(bf16[4,264,256]{2,1,0:T(8,128)(2,1)} %pack.1), calls=%async_computation | async-start | bytes 1081344 | tf_op jit(solution)/shard_map/all_to_all | solution.py:269
  8.9 0.7 %copy-start.2 = (s32[512,1]{0,1:T(1,128)S(1)}, s32[512,1]{0,1:T(1,128)}, u32[]{:S(2)}) copy-start(s32[512,1]{0,1:T(1,128)} %param.10) | copy-start | bytes 6148
  8.9 0.7 %copy-start.1 = (s32[512,1]{0,1:T(1,128)S(1)}, s32[512,1]{0,1:T(1,128)}, u32[]{:S(2)}) copy-start(s32[512,1]{0,1:T(1,128)} %param.8) | copy-start | bytes 6148
  8.9 0.7 %copy-start.3 = (s32[32]{0:T(128)S(1)}, s32[32]{0:T(128)}, u32[]{:S(2)}) copy-start(s32[32]{0:T(128)} %param.11) | copy-start | bytes 388

commit v7 on v6

--- a/solution.py
+++ b/solution.py
@@ -16,6 +16,7 @@
 SCALE_ROWS = 8
 LANES = 128
 CHIPS_SIDE = 4
+SPARE = 6
 
 
 def rotated(count, first):
@@ -52,6 +53,13 @@
         move.start()
     for move in moves:
         move.wait()
+
+
+def three_terms(value):
+    high = value.astype(BF16).astype(F32)
+    rest = value - high
+    middle = rest.astype(BF16).astype(F32)
+    return high, middle, rest - middle
 
 
 def count_kernel(
@@ -212,22 +220,34 @@
         )
     mass = jnp.sum(mass, axis=1, keepdims=True)
     pooled = pooled[:samples] + pooled[samples:]
-    lane = lax.broadcasted_iota(jnp.int32, (samples, LANES), 1)
-    last = jnp.where(lane == 0, peak, mass)
-    size = out_ref.shape[1]
+    high = pooled.astype(BF16)
+    low = pooled - high.astype(F32)
+    lane = lax.broadcasted_iota(jnp.int32, (samples, width), 1)
+    for place, term in enumerate(three_terms(peak) + three_terms(mass)):
+        low = jnp.where(lane == width - SPARE + place, term, low)
+    low = low.astype(BF16)
+    size = out_ref.shape[1] // 2
     for block in range(out_ref.shape[0]):
-        out_ref[block, :, :width] = pooled[block * size : (block + 1) * size]
-        out_ref[block, :, width:] = last[block * size : (block + 1) * size]
+        out_ref[block, :size, :] = high[block * size : (block + 1) * size]
+        out_ref[block, size:, :] = low[block * size : (block + 1) * size]
 
 
 def merge_kernel(got_ref, out_ref):
-    count = got_ref.shape[0]
-    width = got_ref.shape[2] - LANES
-    peaks = [got_ref[k, :, width : width + 1] for k in range(count)]
+    count, height, width = got_ref.shape
+    size = height // 2
+    lane = lax.broadcasted_iota(jnp.int32, (size, width), 1)
+    sums, peaks, masses = [], [], []
+    for k in range(count):
+        low = got_ref[k, size:, :].astype(F32)
+        spare = [low[:, at : at + 1] for at in range(width - SPARE, width)]
+        peaks.append(spare[0] + (spare[1] + spare[2]))
+        masses.append(spare[3] + (spare[4] + spare[5]))
+        low = jnp.where(lane < width - SPARE, low, 0.0)
+        sums.append(got_ref[k, :size, :].astype(F32) + low)
     top = functools.reduce(jnp.maximum, peaks)
     shift = [jnp.exp(peak - top) for peak in peaks]
-    mass = sum(f * got_ref[k, :, width + 1 : width + 2] for k, f in enumerate(shift))
-    pooled = sum(f * got_ref[k, :, :width] for k, f in enumerate(shift)) / mass
+    mass = sum(f * part for f, part in zip(shift, masses))
+    pooled = sum(f * part for f, part in zip(shift, sums)) / mass
     pooled = pooled.astype(BF16)
     for part in range(width // LANES):
         out_ref[:, part, :] = pooled[:, part * LANES : (part + 1) * LANES]
@@ -320,7 +340,7 @@
     query = exchange(masked, across_rows)
     partial = pl.pallas_call(
         pool_kernel,
-        out_shape=jax.ShapeDtypeStruct((side, samples // side, width + LANES), F32),
+        out_shape=jax.ShapeDtypeStruct((side, 2 * (samples // side), width), BF16),
         in_specs=[VMEM, VMEM, VMEM],
         out_specs=VMEM,
         scratch_shapes=[pltpu.VMEM((samples, held), F32)],

time: 55.8 us -> 55.6 us (level)
  no operation moved by 1% of the time
where the time goes in v7:
time: 55.6 us; the launch traced here: 55.3 us
  blocking collectives  39.6 us (71%)
  starting transfers between devices  7.15 us (13%)
  Pallas kernels  6.22 us (11%)
  waiting for transfers between devices  1.51 us (3%)
  local copies, waits for them, and re-layouts  0.7 us (1%)
    all_to_all x3, blocking collectives, exchange(): lax.all_to_all(blocks, ('tbl', 'grp'), 0, 0, axis_index_groups=groups, ti...  39.6 us
    all_to_all x1, starting transfers between devices, exchange(): lax.all_to_all(blocks, ('tbl', 'grp'), 0, 0, axis_index_groups=groups, ti...  7.15 us
    pallas_call x1, Pallas kernels, per_device(): pl.pallas_call(functools.partial(count_kernel, order), out_shape=[jax.Sha...  2.11 us
    pallas_call x1, Pallas kernels, per_device(): pl.pallas_call(pack_kernel, out_shape=jax.ShapeDtypeStruct((side, rows +...  1.76 us
    all_to_all x1, waiting for transfers between devices, exchange(): lax.all_to_all(blocks, ('tbl', 'grp'), 0, 0, axis_index_groups=groups, ti...  1.51 us
  transfers between devices with their start and end apart: 1, of which 1 were waited for; matrix products, arithmetic and copies ran while one was open for 0% of the time, Pallas kernels for 4%

profile of v7, /device:TPU:1, one launch (start us, length us, event | category | flops | bytes accessed | tf_op | source)
XLA Modules:
  0.0 55.3 jit_solution(17958341107192168794)
XLA Ops:
  0.0 1.8 %pack.1 = bf16[4,264,256]{2,1,0:T(8,128)(2,1)} custom-call(bf16[256,256]{1,0:T(8,128)(2,1)} %bitcast.13, f32[1,256]{1,0:T(1,128)} %scales_ref.1), custom_call_target="tpu_custom_call" | custom-call | tf_op jit(solution)/shard_map/pack/pallas_call | solution.py:293
  1.8 0.0 copy-start
  1.8 7.1 %all-to-all-start = ((bf16[4,264,256]{2,1,0:T(8,128)(2,1)}), bf16[4,264,256]{2,1,0:T(8,128)(2,1)S(1)}, u32[]{:S(2)}, u32[]{:S(2)}) async-start(bf16[4,264,256]{2,1,0:T(8,128)(2,1)} %pack.1), calls=%async_computation | async-start | bytes 1081344 | tf_op jit(solution)/shard_map/all_to_all | solution.py:289
  8.9 0.0 copy-start.2
  8.9 0.0 copy-start.1
  8.9 0.0 copy-start.3
  8.9 0.0 copy-done
  8.9 0.7 %copy-done.2 = s32[512,1]{0,1:T(1,128)S(1)} copy-done((s32[512,1]{0,1:T(1,128)S(1)}, s32[512,1]{0,1:T(1,128)}, u32[]{:S(2)}) %copy-start.2) | copy-done | bytes 2072
  9.6 0.0 copy-done.1
  9.6 0.0 copy-done.3
  9.6 2.1 %count.1 = (f32[128,1024]{1,0:T(8,128)S(1)}, f32[128,1024]{1,0:T(8,128)S(1)}, f32[32,32]{1,0:T(8,128)S(1)}) custom-call(s32[1]{0:T(128)} %bitcast.tbl_ref, s32[1]{0:T(128)} %bitcast.1.grp_ref, s32[32,512]{1,0:T(8,128)S(1)} %bitcast.9, s32[1,512]{1,0:T(1,128)S(1)} %bitcast.10, s32[1,512]{1,0:T(1,128)S(1)} %bitcast.11, s32[1,32]{1,0:T(1,128)S(1)} %bitcast.12), custom_call_target="tpu_custom_call" | custom-call | flops 100000000 | bytes 1000000 | tf_op jit(solution)/shard_map/count/pallas_call | solution.py:308
  11.7 1.5 %all-to-all-done.table_ref = bf16[4,264,256]{2,1,0:T(8,128)(2,1)S(1)} async-done(((bf16[4,264,256]{2,1,0:T(8,128)(2,1)}), bf16[4,264,256]{2,1,0:T(8,128)(2,1)S(1)}, u32[]{:S(2)}, u32[]{:S(2)}) %all-to-all-start) | async-done | bytes 540704 | tf_op jit(solution)/shard_map/all_to_all | solution.py:289
  13.3 0.3 query.1
  13.6 8.2 %all_to_all.20.query_ref = bf16[4,136,256]{2,1,0:T(8,128)(2,1)S(1)} all-to-all(bf16[4,136,256]{2,1,0:T(8,128)(2,1)S(1)} %query.1), channel_id=1, replica_groups={{2,3,0,1},{6,7,4,5},{10,11,8,9},{14,15,12,13},{24,28,16,20},{25,29,17,2..., dimensions={0} | all-to-all | bytes 557056 | tf_op jit(solution)/shard_map/all_to_all | solution.py:289
  21.8 0.9 %pool.1 = bf16[4,64,256]{2,1,0:T(8,128)(2,1)S(1)} custom-call(bf16[4,264,256]{2,1,0:T(8,128)(2,1)S(1)} %all-to-all-done.table_ref, f32[128,1024]{1,0:T(8,128)S(1)} %get-tuple-element.9.counts_ref, bf16[4,136,256]{2,1,0:T(8,128)(2,1)S(1)} %all_to_all.20.query_ref), custom_call_target="tpu_custom_call" | custom-call | tf_op jit(solution)/shard_map/pool/pallas_call | solution.py:341
  22.7 7.2 %all_to_all.21.got_ref = bf16[4,64,256]{2,1,0:T(8,128)(2,1)S(1)} all-to-all(bf16[4,64,256]{2,1,0:T(8,128)(2,1)S(1)} %pool.1), channel_id=1, replica_groups={{2,3,0,1},{6,7,4,5},{10,11,8,9},{14,15,12,13},{24,28,16,20},{25,29,17,2..., dimensions={0} | all-to-all | bytes 262144 | tf_op jit(solution)/shard_map/all_to_all | solution.py:289
  29.9 0.3 merge.1
  30.3 24.2 %all_to_all.22.pooled_ref = bf16[32,2,128]{2,1,0:T(2,128)(2,1)S(1)} all-to-all(bf16[32,2,128]{2,1,0:T(2,128)(2,1)S(1)} %merge.1), channel_id=1, replica_groups={{304,320,336,352,368,384,400,416,432,448,464,480,496,0,16,32,48,64,80,9..., dimensions={0} | all-to-all | bytes 32768 | tf_op jit(solution)/shard_map/all_to_all | solution.py:289
  54.5 0.8 %order.1 = bf16[1,32,256]{2,1,0:T(8,128)(2,1)} custom-call(f32[32,32]{1,0:T(8,128)S(1)} %get-tuple-element.8.place_ref, bf16[32,2,128]{2,1,0:T(2,128)(2,1)S(1)} %all_to_all.22.pooled_ref), custom_call_target="tpu_custom_call" | custom-call | tf_op jit(solution)/shard_map/order/pallas_call | solution.py:360
Async XLA Ops:
  1.8 7.2 %copy-start = (s32[512,1,32]{0,2,1:T(8,128)S(1)}, s32[512,1,32]{0,2,1:T(8,128)}, u32[]{:S(2)}) copy-start(s32[512,1,32]{0,2,1:T(8,128)} %param.9) | copy-start | bytes 196612
  1.8 11.5 %all-to-all-start = ((bf16[4,264,256]{2,1,0:T(8,128)(2,1)}), bf16[4,264,256]{2,1,0:T(8,128)(2,1)S(1)}, u32[]{:S(2)}, u32[]{:S(2)}) async-start(bf16[4,264,256]{2,1,0:T(8,128)(2,1)} %pack.1), calls=%async_computation | async-start | bytes 1081344 | tf_op jit(solution)/shard_map/all_to_all | solution.py:289
  8.9 0.7 %copy-start.2 = (s32[512,1]{0,1:T(1,128)S(1)}, s32[512,1]{0,1:T(1,128)}, u32[]{:S(2)}) copy-start(s32[512,1]{0,1:T(1,128)} %param.10) | copy-start | bytes 6148
  8.9 0.7 %copy-start.1 = (s32[512,1]{0,1:T(1,128)S(1)}, s32[512,1]{0,1:T(1,128)}, u32[]{:S(2)}) copy-start(s32[512,1]{0,1:T(1,128)} %param.8) | copy-start | bytes 6148
  8.9 0.7 %copy-start.3 = (s32[32]{0:T(128)S(1)}, s32[32]{0:T(128)}, u32[]{:S(2)}) copy-start(s32[32]{0:T(128)} %param.11) | copy-start | bytes 388

commit v8 on v6

--- a/solution.py
+++ b/solution.py
@@ -252,7 +252,7 @@
     side = CHIPS_SIDE
     samples = tbl_count * side
     held = rows * side
-    tbl_order = rotated(tbl_count, tbl_count // 2 + 3)
+    tbl_order = rotated(tbl_count, tbl_count // 2 + 5)
     side_order = rotated(side, side // 2)
     order = (tbl_order, side_order)
     tables, places = range(tbl_count), range(side)

time: 55.8 us -> 55.8 us (level)
  no operation moved by 1% of the time
where the time goes in v8:
time: 55.8 us; the launch traced here: 55.5 us
  blocking collectives  40 us (72%)
  starting transfers between devices  7.15 us (13%)
  Pallas kernels  6.06 us (11%)
  waiting for transfers between devices  1.51 us (3%)
  local copies, waits for them, and re-layouts  0.7 us (1%)
    all_to_all x3, blocking collectives, exchange(): lax.all_to_all(blocks, ('tbl', 'grp'), 0, 0, axis_index_groups=groups, ti...  40 us
    all_to_all x1, starting transfers between devices, exchange(): lax.all_to_all(blocks, ('tbl', 'grp'), 0, 0, axis_index_groups=groups, ti...  7.15 us
    pallas_call x1, Pallas kernels, per_device(): pl.pallas_call(functools.partial(count_kernel, order), out_shape=[jax.Sha...  2.11 us
    pallas_call x1, Pallas kernels, per_device(): pl.pallas_call(pack_kernel, out_shape=jax.ShapeDtypeStruct((side, rows +...  1.76 us
    all_to_all x1, waiting for transfers between devices, exchange(): lax.all_to_all(blocks, ('tbl', 'grp'), 0, 0, axis_index_groups=groups, ti...  1.51 us
  transfers between devices with their start and end apart: 1, of which 1 were waited for; matrix products, arithmetic and copies ran while one was open for 0% of the time, Pallas kernels for 4%

profile of v8, /device:TPU:1, one launch (start us, length us, event | category | flops | bytes accessed | tf_op | source)
XLA Modules:
  0.0 55.5 jit_solution(8503952499044213217)
XLA Ops:
  0.0 1.8 %pack.1 = bf16[4,264,256]{2,1,0:T(8,128)(2,1)} custom-call(bf16[256,256]{1,0:T(8,128)(2,1)} %bitcast.13, f32[1,256]{1,0:T(1,128)} %scales_ref.1), custom_call_target="tpu_custom_call" | custom-call | tf_op jit(solution)/shard_map/pack/pallas_call | solution.py:273
  1.8 0.0 copy-start
  1.8 7.1 %all-to-all-start = ((bf16[4,264,256]{2,1,0:T(8,128)(2,1)}), bf16[4,264,256]{2,1,0:T(8,128)(2,1)S(1)}, u32[]{:S(2)}, u32[]{:S(2)}) async-start(bf16[4,264,256]{2,1,0:T(8,128)(2,1)} %pack.1), calls=%async_computation | async-start | bytes 1081344 | tf_op jit(solution)/shard_map/all_to_all | solution.py:269
  8.9 0.0 copy-start.2
  8.9 0.0 copy-start.1
  8.9 0.0 copy-start.3
  8.9 0.0 copy-done
  8.9 0.7 %copy-done.2 = s32[512,1]{0,1:T(1,128)S(1)} copy-done((s32[512,1]{0,1:T(1,128)S(1)}, s32[512,1]{0,1:T(1,128)}, u32[]{:S(2)}) %copy-start.2) | copy-done | bytes 2072
  9.6 0.0 copy-done.1
  9.6 0.0 copy-done.3
  9.6 2.1 %count.1 = (f32[128,1024]{1,0:T(8,128)S(1)}, f32[128,1024]{1,0:T(8,128)S(1)}, f32[32,32]{1,0:T(8,128)S(1)}) custom-call(s32[1]{0:T(128)} %bitcast.tbl_ref, s32[1]{0:T(128)} %bitcast.1.grp_ref, s32[32,512]{1,0:T(8,128)S(1)} %bitcast.9, s32[1,512]{1,0:T(1,128)S(1)} %bitcast.10, s32[1,512]{1,0:T(1,128)S(1)} %bitcast.11, s32[1,32]{1,0:T(1,128)S(1)} %bitcast.12), custom_call_target="tpu_custom_call" | custom-call | flops 100000000 | bytes 1000000 | tf_op jit(solution)/shard_map/count/pallas_call | solution.py:288
  11.7 1.5 %all-to-all-done.table_ref = bf16[4,264,256]{2,1,0:T(8,128)(2,1)S(1)} async-done(((bf16[4,264,256]{2,1,0:T(8,128)(2,1)}), bf16[4,264,256]{2,1,0:T(8,128)(2,1)S(1)}, u32[]{:S(2)}, u32[]{:S(2)}) %all-to-all-start) | async-done | bytes 540704 | tf_op jit(solution)/shard_map/all_to_all | solution.py:269
  13.3 0.3 query.1
  13.6 8.2 %all_to_all.20.query_ref = bf16[4,136,256]{2,1,0:T(8,128)(2,1)S(1)} all-to-all(bf16[4,136,256]{2,1,0:T(8,128)(2,1)S(1)} %query.1), channel_id=1, replica_groups={{2,3,0,1},{6,7,4,5},{10,11,8,9},{14,15,12,13},{24,28,16,20},{25,29,17,2..., dimensions={0} | all-to-all | bytes 557056 | tf_op jit(solution)/shard_map/all_to_all | solution.py:269
  21.8 0.9 %pool.1 = f32[4,32,384]{2,1,0:T(8,128)S(1)} custom-call(bf16[4,264,256]{2,1,0:T(8,128)(2,1)S(1)} %all-to-all-done.table_ref, f32[128,1024]{1,0:T(8,128)S(1)} %get-tuple-element.9.counts_ref, bf16[4,136,256]{2,1,0:T(8,128)(2,1)S(1)} %all_to_all.20.query_ref), custom_call_target="tpu_custom_call" | custom-call | tf_op jit(solution)/shard_map/pool/pallas_call | solution.py:321
  22.7 7.5 %all_to_all.21.got_ref = f32[4,32,384]{2,1,0:T(8,128)S(1)} all-to-all(f32[4,32,384]{2,1,0:T(8,128)S(1)} %pool.1), channel_id=1, replica_groups={{2,3,0,1},{6,7,4,5},{10,11,8,9},{14,15,12,13},{24,28,16,20},{25,29,17,2..., dimensions={0} | all-to-all | bytes 393216 | tf_op jit(solution)/shard_map/all_to_all | solution.py:269
  30.2 0.2 merge.1
  30.4 24.3 %all_to_all.22.pooled_ref = bf16[32,2,128]{2,1,0:T(2,128)(2,1)S(1)} all-to-all(bf16[32,2,128]{2,1,0:T(2,128)(2,1)S(1)} %merge.1), channel_id=1, replica_groups={{336,352,368,384,400,416,432,448,464,480,496,0,16,32,48,64,80,96,112,12..., dimensions={0} | all-to-all | bytes 32768 | tf_op jit(solution)/shard_map/all_to_all | solution.py:269
  54.7 0.8 %order.1 = bf16[1,32,256]{2,1,0:T(8,128)(2,1)} custom-call(f32[32,32]{1,0:T(8,128)S(1)} %get-tuple-element.8.place_ref, bf16[32,2,128]{2,1,0:T(2,128)(2,1)S(1)} %all_to_all.22.pooled_ref), custom_call_target="tpu_custom_call" | custom-call | tf_op jit(solution)/shard_map/order/pallas_call | solution.py:340
Async XLA Ops:
  1.8 7.2 %copy-start = (s32[512,1,32]{0,2,1:T(8,128)S(1)}, s32[512,1,32]{0,2,1:T(8,128)}, u32[]{:S(2)}) copy-start(s32[512,1,32]{0,2,1:T(8,128)} %param.9) | copy-start | bytes 196612
  1.8 11.5 %all-to-all-start = ((bf16[4,264,256]{2,1,0:T(8,128)(2,1)}), bf16[4,264,256]{2,1,0:T(8,128)(2,1)S(1)}, u32[]{:S(2)}, u32[]{:S(2)}) async-start(bf16[4,264,256]{2,1,0:T(8,128)(2,1)} %pack.1), calls=%async_computation | async-start | bytes 1081344 | tf_op jit(solution)/shard_map/all_to_all | solution.py:269
  8.9 0.7 %copy-start.2 = (s32[512,1]{0,1:T(1,128)S(1)}, s32[512,1]{0,1:T(1,128)}, u32[]{:S(2)}) copy-start(s32[512,1]{0,1:T(1,128)} %param.10) | copy-start | bytes 6148
  8.9 0.7 %copy-start.1 = (s32[512,1]{0,1:T(1,128)S(1)}, s32[512,1]{0,1:T(1,128)}, u32[]{:S(2)}) copy-start(s32[512,1]{0,1:T(1,128)} %param.8) | copy-start | bytes 6148
  8.9 0.7 %copy-start.3 = (s32[32]{0:T(128)S(1)}, s32[32]{0:T(128)}, u32[]{:S(2)}) copy-start(s32[32]{0:T(128)} %param.11) | copy-start | bytes 388
